TPU v7x, 32 devices: a whole 2x2x4 slice. The times are simulated.
32 devices in a mesh: grp: 4 (over y, x), section: 2 (over core), row: 4 (over z).
Axes of the slice: x: 2, y: 2, z: 4, core: 2. Of those that a mesh axis runs over, the one named last changes fastest.
Arguments:
- matrices: float32 [4, 8192, 8192], P('grp', 'row', 'section'), parts along dimension 0, may hold values from -57 to 57, as said below
Outputs:
- reduced: float32 [4, 8192, 8192], P('grp', 'row', 'section'), parts along dimension 0
There are 4 independent parts, one for each index of `grp`. A program takes and returns all parts, laid end to end along the dimension named above; each array names one. Nothing has to cross between parts.
Inputs may be any that keep to these rules, and one draw needn't show every extreme that they name: `matrices`: each matrix is exactly symmetric.
All inputs are finite; a program needn't handle non-finite values.
Results may differ from a plain program's by a relative error of at most 0.00023.
Values sent between devices are 32-bit elements; how exact they have to be, the bound alone decides.
No kernel may reach another device: no remote copies, remote signals or barrier semaphores. Data moves between devices by JAX's collectives and lax.ppermute only.
A program may use at most 128 MiB of HBM per device.

v0:
```python
import jax
import jax.numpy as jnp
from jax import lax
from jax.sharding import PartitionSpec as P

NB = 8


highest = lax.Precision.HIGHEST


def broadcast(value, axis, source):
    kept = jnp.where(lax.axis_index(axis) == source, value, 0).astype(value.dtype)
    return lax.psum(kept, axis)


def local(matrices):
    height = matrices.shape[1]
    breadth = matrices.shape[2]
    order = height * lax.axis_size("row")
    row_start = lax.axis_index("row") * height
    col_start = lax.axis_index("section") * breadth
    owned = jnp.swapaxes(matrices[:, :, :NB], 1, 2)
    owned = broadcast(owned, "section", 0)
    panel_cols = lax.all_gather(owned, "row", axis=2, tiled=True)
    positions = jnp.arange(order, dtype=jnp.int32)
    left_list = []
    right_list = []
    for column in range(NB):
        current = panel_cols[:, column, :]
        if column > 0:
            lefts = jnp.stack(left_list, 1)
            rights = jnp.stack(right_list, 1)
            current = current - jnp.einsum(
                "mkn,mk->mn", lefts, rights[:, :, column], precision=highest
            )
            current = current - jnp.einsum(
                "mkn,mk->mn", rights, lefts[:, :, column], precision=highest
            )
        below = jnp.where(positions[None, :] > column, current, 0.0)
        length = jnp.sqrt(jnp.sum(below * below, axis=1))
        reflector = below + jnp.where(positions[None, :] == column + 1, length[:, None], 0.0)
        scaling = 2.0 / (jnp.sum(reflector * reflector, axis=1) + 1e-06)
        row_part = lax.dynamic_slice_in_dim(reflector, row_start, height, 1)
        partial_cols = jnp.einsum("mij,mi->mj", matrices, row_part, precision=highest)
        summed_cols = lax.psum(partial_cols, "row")
        image = lax.all_gather(summed_cols, "section", axis=1, tiled=True)
        if column > 0:
            right_dots = jnp.einsum("mkn,mn->mk", rights, reflector, precision=highest)
            left_dots = jnp.einsum("mkn,mn->mk", lefts, reflector, precision=highest)
            image = image - jnp.einsum("mkn,mk->mn", lefts, right_dots, precision=highest)
            image = image - jnp.einsum("mkn,mk->mn", rights, left_dots, precision=highest)
        corrected = scaling[:, None] * image
        inner = jnp.sum(corrected * reflector, axis=1)
        partner = corrected - (0.5 * scaling * inner)[:, None] * reflector
        left_list.append(reflector)
        right_list.append(partner)
    lefts = jnp.stack(left_list, 1)
    rights = jnp.stack(right_list, 1)
    rows_left = lax.dynamic_slice_in_dim(lefts, row_start, height, 2)
    rows_right = lax.dynamic_slice_in_dim(rights, row_start, height, 2)
    cols_left = lax.dynamic_slice_in_dim(lefts, col_start, breadth, 2)
    cols_right = lax.dynamic_slice_in_dim(rights, col_start, breadth, 2)
    reduced = matrices - jnp.einsum("mki,mkj->mij", rows_left, cols_right, precision=highest)
    reduced = reduced - jnp.einsum("mki,mkj->mij", rows_right, cols_left, precision=highest)
    return reduced


def solution(mesh):
    in_specs = (P("grp", "row", "section"),)
    out_specs = P("grp", "row", "section")
    return jax.shard_map(local, mesh=mesh, in_specs=in_specs, out_specs=out_specs, check_vma=False)
```

profile of v0, /device:TPU:0, one launch (start us, length us, event | category | flops | bytes accessed | tf_op | source)
XLA Modules:
  0.0 484.7 jit_solution(7150372267628386064)
XLA Ops:
  6.5 1.3 slice.69
  8.1 0.6 select_bitcast_fusion
  8.8 21.3 %all-reduce.2.cloned.1.call-done = f32[1,8,2048]{2,1,0:T(8,128)} async-done(((f32[1,8,2048]{2,1,0:T(8,128)}), f32[1,8,2048]{2,1,0:T(8,128)}) %all-reduce.2.cloned.1.call-update) | async-done | bytes 65552 | tf_op jit(solution)/shard_map/psum | solution.py:14
  30.1 14.4 %all_gather.27 = f32[1,8,8192]{2,1,0:T(8,128)S(1)} all-gather(f32[1,8,2048]{2,1,0:T(8,128)} %all-reduce.2.cloned.1.call-done), channel_id=1, replica_groups=mesh['grp'=4,'section'=2,'row'=4] {'row'}, dimensions={2}, use_global_device_ids=true | all-gather | bytes 327680 | tf_op jit(solution)/shard_map/all_gather | solution.py:25
  44.5 0.7 multiply_reduce_fusion.25
  45.9 0.7 multiply_reduce_fusion.24
  46.8 0.7 slice.95
  47.4 19.5 %fusion.14 = f32[1,4096]{1,0:T(1,128)S(1)} fusion(f32[1,2048,4096]{2,1,0:T(8,128)} %param.1, f32[1,8192]{1,0:T(1,128)S(1)} %get-tuple-element.26, s32[]{:T(128)S(6)} %select_n.146), kind=kOutput, calls=%fused_computation.16 | convolution fusion | flops 100663296 | bytes 33579012 | tf_op jit(solution)/shard_map/mij,mi->mj/dot_general | solution.py:45
  66.9 19.3 %psum.64 = f32[1,4096]{1,0:T(1,128)S(1)} all-reduce(f32[1,4096]{1,0:T(1,128)S(1)} %fusion.14), channel_id=1, replica_groups=mesh['grp'=4,'section'=2,'row'=4] {'row'}, use_global_device_ids=true, to_apply=%region_3.4 | all-reduce | flops 4096 | bytes 32768 | tf_op jit(solution)/shard_map/psum | solution.py:46
  86.2 1.8 all_gather.28
  88.7 0.7 multiply_reduce_fusion.23
  90.6 1.9 multiply_reduce_fusion.22
  93.2 0.7 multiply_reduce_fusion.21
  94.8 19.5 %fusion.12 = f32[1,4096]{1,0:T(1,128)S(1)} fusion(f32[2048,1]{0,1:T(1,128)S(1)} %bitcast.471, f32[1,2048,4096]{2,1,0:T(8,128)} %param.1), kind=kOutput, calls=%fused_computation.14 | convolution fusion | flops 100663296 | bytes 33579008 | tf_op jit(solution)/shard_map/mij,mi->mj/dot_general | solution.py:45
  114.3 15.5 %psum.65 = f32[1,4096]{1,0:T(1,128)S(1)} all-reduce(f32[1,4096]{1,0:T(1,128)S(1)} %fusion.12), channel_id=1, replica_groups=mesh['grp'=4,'section'=2,'row'=4] {'row'}, use_global_device_ids=true, to_apply=%region_7.8 | all-reduce | flops 4096 | bytes 32768 | tf_op jit(solution)/shard_map/psum | solution.py:46
  129.8 2.3 all_gather.29
  132.2 1.3 broadcast_multiply_fusion.7
  133.4 0.7 multiply_reduce_fusion.20
  135.8 0.6 multiply_reduce_fusion.19
  137.1 0.6 multiply_reduce_fusion.18
  137.7 0.7 convolution_bitcast_fusion.10
  138.4 0.7 convolution_bitcast_fusion.11
  139.8 19.5 %fusion.10 = f32[1,4096]{1,0:T(1,128)S(1)} fusion(f32[2048,1]{0,1:T(1,128)S(1)} %bitcast.466, f32[1,2048,4096]{2,1,0:T(8,128)} %param.1), kind=kOutput, calls=%fused_computation.12 | convolution fusion | flops 100663296 | bytes 33579008 | tf_op jit(solution)/shard_map/mij,mi->mj/dot_general | solution.py:45
  159.3 16.3 %psum.66 = f32[1,4096]{1,0:T(1,128)S(1)} all-reduce(f32[1,4096]{1,0:T(1,128)S(1)} %fusion.10), channel_id=1, replica_groups=mesh['grp'=4,'section'=2,'row'=4] {'row'}, use_global_device_ids=true, to_apply=%region_11.12 | all-reduce | flops 4096 | bytes 32768 | tf_op jit(solution)/shard_map/psum | solution.py:46
  175.6 2.0 all_gather.30
  178.0 1.0 multiply_reduce_fusion.17
  181.2 0.6 multiply_reduce_fusion.16
  182.5 0.6 multiply_reduce_fusion.15
  183.1 0.7 convolution_bitcast_fusion.8
  183.8 0.7 convolution_bitcast_fusion.9
  185.2 19.5 %fusion.8 = f32[1,4096]{1,0:T(1,128)S(1)} fusion(f32[2048,1]{0,1:T(1,128)S(1)} %bitcast.467, f32[1,2048,4096]{2,1,0:T(8,128)} %param.1), kind=kOutput, calls=%fused_computation.10 | convolution fusion | flops 100663296 | bytes 33579008 | tf_op jit(solution)/shard_map/mij,mi->mj/dot_general | solution.py:45
  204.7 15.6 %psum.67 = f32[1,4096]{1,0:T(1,128)S(1)} all-reduce(f32[1,4096]{1,0:T(1,128)S(1)} %fusion.8), channel_id=1, replica_groups=mesh['grp'=4,'section'=2,'row'=4] {'row'}, use_global_device_ids=true, to_apply=%region_15.16 | all-reduce | flops 4096 | bytes 32768 | tf_op jit(solution)/shard_map/psum | solution.py:46
  220.2 2.0 all_gather.31
  222.7 1.1 multiply_reduce_fusion.14
  227.1 0.6 multiply_reduce_fusion.12
  227.7 0.7 convolution_bitcast_fusion.6
  228.4 0.7 convolution_bitcast_fusion.7
  229.8 19.5 %fusion.6 = f32[1,4096]{1,0:T(1,128)S(1)} fusion(f32[2048,1]{0,1:T(1,128)S(1)} %bitcast.468, f32[1,2048,4096]{2,1,0:T(8,128)} %param.1), kind=kOutput, calls=%fused_computation.8 | convolution fusion | flops 100663296 | bytes 33579008 | tf_op jit(solution)/shard_map/mij,mi->mj/dot_general | solution.py:45
  249.3 16.3 %psum.68 = f32[1,4096]{1,0:T(1,128)S(1)} all-reduce(f32[1,4096]{1,0:T(1,128)S(1)} %fusion.6), channel_id=1, replica_groups=mesh['grp'=4,'section'=2,'row'=4] {'row'}, use_global_device_ids=true, to_apply=%region_19.20 | all-reduce | flops 4096 | bytes 32768 | tf_op jit(solution)/shard_map/psum | solution.py:46
  265.6 2.1 all_gather.32
  268.0 1.0 multiply_reduce_fusion.11
  272.6 0.6 multiply_reduce_fusion.9
  273.2 0.7 convolution_bitcast_fusion.4
  273.9 0.7 convolution_bitcast_fusion.5
  275.3 19.5 %fusion.4 = f32[1,4096]{1,0:T(1,128)S(1)} fusion(f32[2048,1]{0,1:T(1,128)S(1)} %bitcast.469, f32[1,2048,4096]{2,1,0:T(8,128)} %param.1), kind=kOutput, calls=%fused_computation.6 | convolution fusion | flops 100663296 | bytes 33579008 | tf_op jit(solution)/shard_map/mij,mi->mj/dot_general | solution.py:45
  294.8 15.6 %psum.69 = f32[1,4096]{1,0:T(1,128)S(1)} all-reduce(f32[1,4096]{1,0:T(1,128)S(1)} %fusion.4), channel_id=1, replica_groups=mesh['grp'=4,'section'=2,'row'=4] {'row'}, use_global_device_ids=true, to_apply=%region_23.24 | all-reduce | flops 4096 | bytes 32768 | tf_op jit(solution)/shard_map/psum | solution.py:46
  310.4 2.1 all_gather.33
  312.8 1.0 multiply_reduce_fusion.8
  317.5 0.6 multiply_reduce_fusion.6
  318.1 0.7 convolution_bitcast_fusion.2
  318.8 0.7 convolution_bitcast_fusion.3
  320.2 19.5 %fusion.2 = f32[1,4096]{1,0:T(1,128)S(1)} fusion(f32[2048,1]{0,1:T(1,128)S(1)} %bitcast.470, f32[1,2048,4096]{2,1,0:T(8,128)} %param.1), kind=kOutput, calls=%fused_computation.4 | convolution fusion | flops 100663296 | bytes 33579008 | tf_op jit(solution)/shard_map/mij,mi->mj/dot_general | solution.py:45
  339.7 16.2 %psum.70 = f32[1,4096]{1,0:T(1,128)S(1)} all-reduce(f32[1,4096]{1,0:T(1,128)S(1)} %fusion.2), channel_id=1, replica_groups=mesh['grp'=4,'section'=2,'row'=4] {'row'}, use_global_device_ids=true, to_apply=%region_27.28 | all-reduce | flops 4096 | bytes 32768 | tf_op jit(solution)/shard_map/psum | solution.py:46
  355.9 2.3 all_gather.34
  358.6 1.0 multiply_reduce_fusion.5
  363.4 0.6 multiply_reduce_fusion.3
  364.0 0.7 convolution_bitcast_fusion
  364.7 0.7 convolution_bitcast_fusion.1
  366.1 19.5 %fusion = f32[1,4096]{1,0:T(1,128)S(1)} fusion(f32[2048,1]{0,1:T(1,128)S(1)} %bitcast.465, f32[1,2048,4096]{2,1,0:T(8,128)} %param.1), kind=kOutput, calls=%fused_computation.2 | convolution fusion | flops 100663296 | bytes 33579008 | tf_op jit(solution)/shard_map/mij,mi->mj/dot_general | solution.py:45
  385.6 15.6 %psum.71 = f32[1,4096]{1,0:T(1,128)S(1)} all-reduce(f32[1,4096]{1,0:T(1,128)S(1)} %fusion), channel_id=1, replica_groups=mesh['grp'=4,'section'=2,'row'=4] {'row'}, use_global_device_ids=true, to_apply=%region_31.32 | all-reduce | flops 4096 | bytes 32768 | tf_op jit(solution)/shard_map/psum | solution.py:46
  401.2 2.0 all_gather.35
  403.5 1.0 multiply_reduce_fusion.2
  406.0 30.3 %fusion.47 = f32[2048,4096]{1,0:T(8,128)} fusion(f32[1,8,8192]{2,1,0:T(8,128)S(1)} %stack.172, s32[]{:T(128)S(6)} %select_n.161, f32[1,8,8192]{2,1,0:T(8,128)S(1)} %stack.84, s32[]{:T(128)S(6)} %select_n.146), kind=kOutput, calls=%fused_computation.77 | convolution fusion | flops 805306368 | bytes 33751048 | tf_op jit(solution)/shard_map/mki,mkj->mij/dot_general | solution.py:64
  436.3 41.3 %bitcast_subtract_fusion = f32[1,2048,4096]{2,1,0:T(8,128)} fusion(f32[1,2048,4096]{2,1,0:T(8,128)} %param.1, f32[2048,4096]{1,0:T(8,128)} %fusion.47, f32[1,8,8192]{2,1,0:T(8,128)S(1)} %stack.84, s32[]{:T(128)S(6)} %select_n.161, f32[1,8,8192]{2,1,0:T(8,128)S(1)} %stack.172, s32[]{:T(128)S(6)} %select_n.146), kind=kOutput, calls=%fused_computation | convolution fusion | flops 822083584 | bytes 100859912 | tf_op jit(solution)/shard_map/mki,mkj->mij/dot_general | solution.py:65
  (73 shorter events, 15.7 us)
Async XLA Ops:
  6.5 23.6 %all-reduce.2.cloned.1.call-start = ((), (), s32[]{:S(2)}) async-start(), calls=%async_computation | async-start | bytes 131072 | tf_op jit(solution)/shard_map/psum | solution.py:14
Sparse Core Ops, SparseCore 0:
  9.6 20.4 all-reduce.1
where the time goes:
time: 492 us; the launch traced here: 485 us
  matrix products  249 us (51%)
  blocking collectives  161 us (33%)
  between operations  30.3 us (6%)
  waiting for transfers between devices  21.3 us (4%)
  other arithmetic  15.9 us (3%)
  local copies, waits for them, and re-layouts  7.2 us (1%)
    dot_general x8, matrix products, local(): jnp.einsum('mij,mi->mj', matrices, row_part, precision=highest)  156 us
    psum x8, blocking collectives, local(): summed_cols = lax.psum(partial_cols, 'row')  130 us
    dot_general x1, matrix products, local(): jnp.einsum('mki,mkj->mij', rows_right, cols_left, precision=highest)  41.3 us
    dot_general x1, matrix products, local(): jnp.einsum('mki,mkj->mij', rows_left, cols_right, precision=highest)  30.3 us
    psum x1, waiting for transfers between devices, broadcast(): return lax.psum(kept, axis)  21.3 us
    all_gather x8, blocking collectives, local(): image = lax.all_gather(summed_cols, 'section', axis=1, tiled=True)  16.7 us
    all_gather x1, blocking collectives, local(): panel_cols = lax.all_gather(owned, 'row', axis=2, tiled=True)  14.4 us
  transfers between devices with their start and end apart: 1, of which 1 were waited for; matrix products, arithmetic and copies ran while one was open for 0% of the time, Pallas kernels for 0%

commit v1 on v0

v1 whole, which is shorter than its diff:
```python
import functools

import jax
import jax.numpy as jnp
from jax import lax
from jax.experimental import pallas as pl
from jax.experimental.pallas import tpu as pltpu
from jax.sharding import PartitionSpec as P

NB = 8
LANES = 128
SUBLANES = 8
MIB = 1 << 20

VMEM = pltpu.VMEM
f32 = jnp.float32
bf16 = jnp.bfloat16


def call(body, outs, args, scratch=(), flops=0, moved=0, limit=15 * MIB, pinned=(), name=None):
    specs = []
    operands = []
    for index, arg in enumerate(args):
        if index in pinned:
            arg = pltpu.with_memory_space_constraint(arg, VMEM)
        specs.append(pl.BlockSpec(memory_space=VMEM))
        operands.append(arg)
    return pl.pallas_call(
        body,
        out_shape=outs,
        in_specs=specs,
        out_specs=jax.tree.map(lambda _: pl.BlockSpec(memory_space=VMEM), outs),
        scratch_shapes=list(scratch),
        compiler_params=pltpu.CompilerParams(vmem_limit_bytes=limit),
        cost_estimate=pl.CostEstimate(flops=flops, bytes_accessed=moved, transcendentals=0),
        name=name,
    )(*operands)


def out(*shape):
    return jax.ShapeDtypeStruct(shape, f32)


def load_body(src, dst, sems, *, pieces):
    rows = src.shape[0] // pieces
    copies = []
    for k in range(pieces):
        part = pl.ds(k * rows, rows)
        copies.append(pltpu.make_async_copy(src.at[part], dst.at[part], sems.at[k]))
    for copy in copies:
        copy.start()
    for copy in copies:
        copy.wait()


def load(block):
    pieces = 8
    return pl.pallas_call(
        functools.partial(load_body, pieces=pieces),
        out_shape=VMEM(block.shape, f32),
        in_specs=[pl.BlockSpec(memory_space=pl.ANY)],
        out_specs=pl.BlockSpec(memory_space=VMEM),
        scratch_shapes=[pltpu.SemaphoreType.DMA((pieces,))],
        compiler_params=pltpu.CompilerParams(vmem_limit_bytes=15 * MIB),
        cost_estimate=pl.CostEstimate(
            flops=4 * 10**8, bytes_accessed=2 * block.size * 4, transcendentals=0
        ),
        name="load",
    )(pltpu.with_memory_space_constraint(block, pltpu.HBM))


def panel_body(src, dst, tall, sem, *, tiles):
    copy = pltpu.make_async_copy(src.at[:, pl.ds(0, LANES)], tall, sem)
    copy.start()
    copy.wait()
    for t in range(tiles):
        turned = tall[pl.ds(t * LANES, LANES), :].T
        dst[pl.ds(t, NB, stride=tiles), :] = turned[:NB, :]


def panel(block):
    height = block.shape[0]
    tiles = height // LANES
    return pl.pallas_call(
        functools.partial(panel_body, tiles=tiles),
        out_shape=out(NB * tiles, LANES),
        in_specs=[pl.BlockSpec(memory_space=pl.ANY)],
        out_specs=pl.BlockSpec(memory_space=VMEM),
        scratch_shapes=[VMEM((height, LANES), f32), pltpu.SemaphoreType.DMA],
        compiler_params=pltpu.CompilerParams(vmem_limit_bytes=2 * MIB),
        cost_estimate=pl.CostEstimate(flops=10**7, bytes_accessed=2 * MIB, transcendentals=0),
        name="panel",
    )(pltpu.with_memory_space_constraint(block, pltpu.HBM))


def gather_panel_body(*refs, count, sections, tiles):
    dst = refs[-1]
    row = lax.axis_index("row")
    section = lax.axis_index("section")
    own = refs[:count]
    other = refs[count:-1]
    total = tiles * count
    for k in range(count):
        place = lax.rem(row + k, count) * tiles
        for column in range(NB):
            part = pl.ds(column * tiles, tiles)
            value = own[k][part, :]
            if sections == 2:
                value = jnp.where(section == 0, value, other[k][part, :])
            dst[pl.ds(pl.multiple_of(column * total + place, SUBLANES), tiles), :] = value


def total_of(value):
    return jnp.sum(jnp.sum(value, axis=0, keepdims=True), axis=1, keepdims=True)


def place_of(shape):
    return lax.broadcasted_iota(jnp.int32, shape, 0) * LANES + lax.broadcasted_iota(
        jnp.int32, shape, 1
    )


def reflect(current, column):
    place = place_of(current.shape)
    rest = jnp.where(place > column + 1, current, 0.0)
    tail = total_of(rest * rest)
    head = current[0:1, column + 1 : column + 2]
    length = jnp.sqrt(tail + head * head)
    head = head + length
    reflector = jnp.where(place == column + 1, head, rest)
    scaling = 2.0 / (tail + head * head + 1e-06)
    return reflector, scaling, head


def multiply(block, vector, part, wide, *, breadth):
    height = block.shape[0]
    pieces = breadth // LANES
    start = lax.axis_index("section") * pieces
    entries = [vector[pl.ds(start + c, SUBLANES, stride=0), :] for c in range(pieces)]

    def turn(t):
        turned = wide[...].T
        part[pl.ds(t, 1), :] = jnp.sum(turned, axis=0, keepdims=True)

    def step(t, carry):
        @pl.when(t > 0)
        def _():
            turn(t - 1)

        for g in range(LANES // SUBLANES):
            rows = pl.ds(pl.multiple_of(t * LANES + g * SUBLANES, SUBLANES), SUBLANES)
            sums = [None, None]
            for c in range(pieces):
                term = block[rows, pl.ds(c * LANES, LANES)] * entries[c]
                sums[c % 2] = term if sums[c % 2] is None else sums[c % 2] + term
            wide[pl.ds(g * SUBLANES, SUBLANES), :] = sums[0] + sums[1]
        return carry

    lax.fori_loop(0, height // LANES, step, 0)
    turn(height // LANES - 1)


def first_body(panel_ref, block, reflector_ref, facts_ref, part, wide, *, breadth):
    rows = reflector_ref.shape[0]
    reflector, scaling, head = reflect(panel_ref[pl.ds(0, rows), :], 0)
    reflector_ref[...] = reflector
    facts_ref[pl.ds(0, 1), :] = jnp.broadcast_to(scaling, (1, LANES))
    facts_ref[pl.ds(1, 1), :] = jnp.broadcast_to(head, (1, LANES))
    multiply(block, reflector_ref, part, wide, breadth=breadth)


def finish_image(pieces, offset, reflector, facts, image_ref):
    count = len(pieces)
    row = lax.axis_index("row")
    for k, piece in enumerate(pieces):
        tiles = piece.shape[0]
        place = lax.rem(row + k, count) * tiles
        image_ref[pl.ds(pl.multiple_of(place, SUBLANES), tiles), :] = piece[...]
    image = image_ref[...]
    if offset is not None:
        image = image - offset[...]
    scaling = facts[0:1, 0:1]
    corrected = scaling * image
    inner = total_of(corrected * reflector)
    return corrected - (0.5 * scaling * inner) * reflector


def step_body(*refs, column, count, breadth):
    pieces = refs[:count]
    refs = refs[count:]
    if column > 1:
        offset, *refs = refs
    else:
        offset = None
    base, old, facts, block, partner_ref, reflector_ref, facts_ref, part, image, wide = refs
    before = old[...]
    partner = finish_image(pieces, offset, before, facts, image)
    partner_ref[...] = partner
    if column == 1:
        base_value = base[pl.ds(old.shape[0], old.shape[0]), :]
    else:
        base_value = base[...]
    current = base_value - before * partner[0:1, column : column + 1] - partner * facts[1:2, 0:1]
    reflector, scaling, head = reflect(current, column)
    reflector_ref[...] = reflector
    facts_ref[pl.ds(0, 1), :] = jnp.broadcast_to(scaling, (1, LANES))
    facts_ref[pl.ds(1, 1), :] = jnp.broadcast_to(head, (1, LANES))
    multiply(block, reflector_ref, part, wide, breadth=breadth)


def between_body(*refs, column):
    lefts = refs[:column]
    rights = refs[column : 2 * column]
    panel_ref, new, offset_ref = refs[2 * column : 2 * column + 3]
    reflector = new[...]
    rows = reflector.shape[0]
    offset = None
    for left, right in zip(lefts, rights):
        left = left[...]
        right = right[...]
        term = left * total_of(right * reflector) + right * total_of(left * reflector)
        offset = term if offset is None else offset + term
    offset_ref[...] = offset
    after = column + 1
    if after < NB:
        base_ref = refs[-1]
        base = panel_ref[pl.ds(after * rows, rows), :]
        for left, right in zip(lefts, rights):
            left = left[...]
            right = right[...]
            base = base - left * right[0:1, after : after + 1]
            base = base - right * left[0:1, after : after + 1]
        base_ref[...] = base


def add_body(a, b, c):
    c[...] = a[...] + b[...]


def split(value):
    high = value.astype(bf16).astype(f32)
    rest = value - high
    middle = rest.astype(bf16).astype(f32)
    low = (rest - middle).astype(bf16).astype(f32)
    return high, middle, low


def last_body(*refs, count, breadth, slots, tall):
    pieces = refs[:count]
    refs = refs[count:]
    lefts = refs[:NB]
    rights = refs[NB : 2 * NB - 1]
    offset, facts, block, dst, image, stack, right_side, left_side, buffer, sems = refs[2 * NB - 1 :]
    total = image.shape[0]
    height = block.shape[0]
    last = lefts[-1][...]
    partner = finish_image(pieces, offset, last, facts, image)
    for k in range(NB):
        stack[pl.ds(k * total, total), :] = lefts[k][...]
        stack[pl.ds((NB + k) * total, total), :] = partner if k == NB - 1 else rights[k][...]
        stack[pl.ds((2 * NB + k) * total, total), :] = lefts[k][...]
    col_start = lax.axis_index("section") * (breadth // LANES)
    row_start = lax.axis_index("row") * (height // LANES)
    pair = 2 * NB

    for c in range(breadth // LANES):
        rows = stack[pl.ds(NB * total + col_start + c, pair, stride=total), :]
        high, middle, low = split(rows)
        group = jnp.concatenate([high, middle, high, middle, low, high, high * 0.0, high * 0.0], 0)
        right_side[:, pl.ds(c * LANES, LANES)] = group.astype(bf16)

    turns = tall // LANES
    steps = height // tall

    def copy_out(step, slot):
        return pltpu.make_async_copy(
            buffer.at[slot], dst.at[pl.ds(pl.multiple_of(step * tall, tall), tall)], sems.at[slot]
        )

    def step(t, carry):
        slot = lax.rem(t, slots)
        for u in range(turns):
            rows = stack[pl.ds(row_start + t * turns + u, pair, stride=total), :]
            high, middle, low = split(rows)
            group = jnp.concatenate(
                [high, high, middle, middle, high, low, high * 0.0, high * 0.0], 0
            )
            left_side[pl.ds(u * LANES, LANES), :] = group.T.astype(bf16)

        @pl.when(t >= slots)
        def _():
            copy_out(t - slots, slot).wait()

        rows = pl.ds(pl.multiple_of(t * tall, tall), tall)
        wide = 512 if breadth % 512 == 0 else LANES
        for c in range(breadth // wide):
            cols = pl.ds(c * wide, wide)
            change = jnp.dot(left_side[...], right_side[:, cols], preferred_element_type=f32)
            buffer[slot, :, cols] = block[rows, cols] - change
        copy_out(t, slot).start()
        return carry

    lax.fori_loop(0, steps, step, 0)
    for t in range(max(0, steps - slots), steps):
        copy_out(t, t % slots).wait()


def turn_by(axis, size, shift):
    return [(i, (i + shift) % size) for i in range(size)]


def local(matrices):
    height, breadth = matrices.shape[1:]
    count = lax.axis_size("row")
    sections = lax.axis_size("section")
    total = count * height // LANES
    tiles = height // LANES
    direct = count <= 4 and sections == 2
    block = matrices.reshape(height, breadth)

    def rows_of(value):
        got = {}
        for k in range(1, count):
            got[k] = lax.ppermute(value, "row", turn_by("row", count, count - k))
        return [value] + [got[k] for k in range(1, count)]

    def swap(value):
        return lax.ppermute(value, "section", [(0, 1), (1, 0)])

    def exchange(part):
        if direct:
            part = call(add_body, out(*part.shape), [part, swap(part)], limit=2 * MIB, name="add")
            return rows_of(part)
        part = lax.psum(part, "section")
        return [lax.all_gather(part, "row", axis=0, tiled=True)]

    own = panel(block)
    if direct:
        kept = rows_of(own)
        kept = kept + [swap(value) for value in kept]
        body = functools.partial(gather_panel_body, count=count, sections=2, tiles=tiles)
        columns = call(body, out(NB * total, LANES), kept, limit=2 * MIB, name="lay")
    else:
        own = jnp.where(lax.axis_index("section") == 0, own, 0.0)
        own = lax.psum(own, "section").reshape(NB, tiles, LANES)
        columns = lax.all_gather(own, "row", axis=1, tiled=True).reshape(NB * total, LANES)
    resident = block

    vector = out(total, LANES)
    facts_shape = out(SUBLANES, LANES)
    part_shape = out(tiles, LANES)
    square = VMEM((LANES, LANES), f32)
    work = 2 * height * breadth

    lefts = []
    rights = []
    left, facts, part = call(
        functools.partial(first_body, breadth=breadth),
        [vector, facts_shape, part_shape],
        [columns, resident],
        scratch=[square],
        flops=work,
        limit=15 * MIB,
        pinned=(1,),
        name="first",
    )
    lefts.append(left)
    offset = None
    base = columns
    for column in range(1, NB):
        pieces = exchange(part)
        args = list(pieces)
        if offset is not None:
            args.append(offset)
        args += [base, lefts[-1], facts, resident]
        right, left, facts, part = call(
            functools.partial(step_body, column=column, count=len(pieces), breadth=breadth),
            [vector, vector, facts_shape, part_shape],
            args,
            scratch=[VMEM((total, LANES), f32), square],
            flops=work,
            limit=15 * MIB,
            pinned=(len(args) - 1,),
            name="step%d" % column,
        )
        rights.append(right)
        outs = [vector, vector] if column + 1 < NB else [vector]
        done = call(
            functools.partial(between_body, column=column),
            outs,
            lefts + rights + [columns, left],
            flops=10**6, limit=2 * MIB,
            name="between%d" % column,
        )
        offset = done[0]
        base = done[-1]
        lefts.append(left)
    pieces = exchange(part)
    slots = 3
    tall = min(256, height)
    operands = list(pieces) + lefts + rights + [offset, facts]
    reduced = pl.pallas_call(
        functools.partial(
            last_body, count=len(pieces), breadth=breadth, slots=slots, tall=tall
        ),
        out_shape=out(height, breadth),
        in_specs=[pl.BlockSpec(memory_space=VMEM)] * (len(operands) + 1),
        out_specs=pl.BlockSpec(memory_space=pl.ANY),
        scratch_shapes=[
            VMEM((total, LANES), f32),
            VMEM((3 * NB * total, LANES), f32),
            VMEM((LANES, breadth), bf16),
            VMEM((tall, LANES), bf16),
            VMEM((slots, tall, breadth), f32),
            pltpu.SemaphoreType.DMA((slots,)),
        ],
        compiler_params=pltpu.CompilerParams(vmem_limit_bytes=15 * MIB),
        cost_estimate=pl.CostEstimate(
            flops=work * 16, bytes_accessed=2 * height * breadth * 4, transcendentals=0
        ),
        name="last",
    )(*operands, pltpu.with_memory_space_constraint(resident, VMEM))
    return reduced.reshape(matrices.shape)


def solution(mesh):
    spec = P("grp", "row", "section")
    return jax.shard_map(local, mesh=mesh, in_specs=(spec,), out_specs=spec, check_vma=False)
```

time: 492 us -> 126 us (0.26); the launches traced: 485 us -> 126 us
  matrix products: 249 us -> 0 us
  blocking collectives: 161 us -> 0 us
  Pallas kernels: 0 us -> 50.4 us
  starting transfers between devices: 0.01 us -> 40.1 us
  between operations: 30.3 us -> 0.23 us
  other arithmetic: 15.9 us -> 0 us
  waiting for transfers between devices: 21.3 us -> 35.2 us
  local copies, waits for them, and re-layouts: 7.2 us -> 0.01 us
    dot_general x46 -> x0, matrix products: 249 us -> none  [the longest x8 156 us: local(): jnp.einsum('mij,mi->mj', matrices, row_part, precision=highest)]
    psum x8 -> x0, blocking collectives: 130 us -> none  [local(): summed_cols = lax.psum(partial_cols, 'row')]
    pallas_call x0 -> x26, Pallas kernels: none -> 50.4 us  [the longest x24 36.5 us: call(): pl.pallas_call(body, out_shape=outs, in_specs=specs, out_specs=jax.tree.m...]
    ppermute x0 -> x39, starting transfers between devices: none -> 40.1 us  [the longest x27 38.9 us: rows_of(): got[k] = lax.ppermute(value, 'row', turn_by('row', count, count - k))]
    ppermute x0 -> x39, waiting for transfers between devices: none -> 35.2 us  [the longest x27 25.3 us: rows_of(): got[k] = lax.ppermute(value, 'row', turn_by('row', count, count - k))]
    all_gather x9 -> x0, blocking collectives: 31.1 us -> none  [the longest x8 16.7 us: local(): image = lax.all_gather(summed_cols, 'section', axis=1, tiled=True)]
    psum x1 -> x0, waiting for transfers between devices: 21.3 us -> none  [broadcast(): return lax.psum(kept, axis)]
    reduce_sum x18 -> x0, other arithmetic: 12.7 us -> none  [the longest x8 6.27 us: local(): length = jnp.sqrt(jnp.sum(below * below, axis=1))]
  transfers between devices with their start and end apart: 1 -> 39, of which waited for: 1 -> 36; matrix products, arithmetic and copies ran while one was open for 0% -> 0% of each run, Pallas kernels for 0% -> 1%
where the time goes in v1:
time: 126 us
  Pallas kernels  50.4 us (40%)
  starting transfers between devices  40.1 us (32%)
  waiting for transfers between devices  35.2 us (28%)
    ppermute x27, starting transfers between devices, rows_of(): got[k] = lax.ppermute(value, 'row', turn_by('row', count, count - k))  38.9 us
    pallas_call x24, Pallas kernels, call(): pl.pallas_call(body, out_shape=outs, in_specs=specs, out_specs=jax.tree.m...  36.5 us
    ppermute x27, waiting for transfers between devices, rows_of(): got[k] = lax.ppermute(value, 'row', turn_by('row', count, count - k))  25.3 us
    pallas_call x1, Pallas kernels, local(): pl.pallas_call(functools.partial(last_body, count=len(pieces), breadth=br...  12.2 us
    ppermute x12, waiting for transfers between devices, swap(): return lax.ppermute(value, 'section', [(0, 1), (1, 0)])  9.97 us
  transfers between devices with their start and end apart: 39, of which 36 were waited for; matrix products, arithmetic and copies ran while one was open for 0% of the time, Pallas kernels for 1%

profile of v1, /device:TPU:0, one launch (start us, length us, event | category | flops | bytes accessed | tf_op | source)
XLA Modules:
  0.0 126.0 jit_solution(4813535574088540040)
XLA Ops:
  0.0 1.7 %panel.1.refs_0_ = f32[128,128]{1,0:T(8,128)S(1)} custom-call(f32[2048,4096]{1,0:T(8,128)} %bitcast.2), custom_call_target="tpu_custom_call" | custom-call | flops 10000000 | bytes 2097152 | tf_op jit(solution)/shard_map/panel/pallas_call | solution.py:84
  1.7 3.1 %collective-permute-start.2 = (f32[128,128]{1,0:T(8,128)S(1)}, f32[128,128]{1,0:T(8,128)S(1)}, u32[]{:S(2)}, u32[]{:S(2)}) collective-permute-start(f32[128,128]{1,0:T(8,128)S(1)} %panel.1.refs_0_), channel_id=1, source_target_pairs={{0,1},{1,2},{2,3},{3,0},{4,5},{5,6},{6,7},{7,4},{8,9},{9,10},{10,1... | collective-permute-start | bytes 196616 | tf_op jit(solution)/shard_map/ppermute | solution.py:324
  4.8 2.6 %collective-permute-start.1 = (f32[128,128]{1,0:T(8,128)S(1)}, f32[128,128]{1,0:T(8,128)S(1)}, u32[]{:S(2)}, u32[]{:S(2)}) collective-permute-start(f32[128,128]{1,0:T(8,128)S(1)} %panel.1.refs_0_), channel_id=1, source_target_pairs={{0,2},{1,3},{2,0},{3,1},{4,6},{5,7},{6,4},{7,5},{8,10},{9,11},{10,... | collective-permute-start | bytes 196616 | tf_op jit(solution)/shard_map/ppermute | solution.py:324
  7.4 1.3 %collective-permute-start = (f32[128,128]{1,0:T(8,128)S(1)}, f32[128,128]{1,0:T(8,128)S(1)}, u32[]{:S(2)}, u32[]{:S(2)}) collective-permute-start(f32[128,128]{1,0:T(8,128)S(1)} %panel.1.refs_0_), channel_id=1, source_target_pairs={{0,3},{1,0},{2,1},{3,2},{4,7},{5,4},{6,5},{7,6},{8,11},{9,8},{10,9... | collective-permute-start | bytes 196616 | tf_op jit(solution)/shard_map/ppermute | solution.py:324
  9.3 2.6 %collective-permute-done.1.refs_2_ = f32[128,128]{1,0:T(8,128)S(1)} collective-permute-done((f32[128,128]{1,0:T(8,128)S(1)}, f32[128,128]{1,0:T(8,128)S(1)}, u32[]{:S(2)}, u32[]{:S(2)}) %collective-permute-start.1) | collective-permute-done | bytes 65568 | tf_op jit(solution)/shard_map/ppermute | solution.py:324
  12.4 0.7 collective-permute-done.5.refs_6_
  13.4 4.2 %first.1 = (f32[64,128]{1,0:T(8,128)S(1)}, f32[8,128]{1,0:T(8,128)S(1)}, f32[16,128]{1,0:T(8,128)S(1)}) custom-call(f32[512,128]{1,0:T(8,128)S(1)} %lay.1.panel_ref.refs_4_.refs_2_.refs_6_.refs_8_.refs_10_.refs_12_.refs_14_, f32[2048,4096]{1,0:T(8,128)S(1)} %bitcast.3), custom_call_target="tpu_custom_call" | custom-call | flops 16777216 | tf_op jit(solution)/shard_map/first/pallas_call | solution.py:28
  18.0 0.9 collective-permute-done.7.b
  18.9 1.6 %collective-permute-start.10 = (f32[16,128]{1,0:T(8,128)S(1)}, f32[16,128]{1,0:T(8,128)S(1)}, u32[]{:S(2)}, u32[]{:S(2)}) collective-permute-start(f32[16,128]{1,0:T(8,128)S(1)} %add.8.refs_0_), channel_id=1, source_target_pairs={{0,1},{1,2},{2,3},{3,0},{4,5},{5,6},{6,7},{7,4},{8,9},{9,10},{10,1... | collective-permute-start | bytes 24584 | tf_op jit(solution)/shard_map/ppermute | solution.py:324
  20.5 2.2 %collective-permute-start.9 = (f32[16,128]{1,0:T(8,128)S(1)}, f32[16,128]{1,0:T(8,128)S(1)}, u32[]{:S(2)}, u32[]{:S(2)}) collective-permute-start(f32[16,128]{1,0:T(8,128)S(1)} %add.8.refs_0_), channel_id=1, source_target_pairs={{0,2},{1,3},{2,0},{3,1},{4,6},{5,7},{6,4},{7,5},{8,10},{9,11},{10,... | collective-permute-start | bytes 24584 | tf_op jit(solution)/shard_map/ppermute | solution.py:324
  22.6 0.7 collective-permute-start.8
  23.3 1.0 collective-permute-done.10.refs_3_
  24.3 0.7 collective-permute-done.9.refs_2_
  25.1 1.2 collective-permute-done.8.refs_1_
  26.3 4.5 %step1.1 = (f32[64,128]{1,0:T(8,128)S(1)}, f32[64,128]{1,0:T(8,128)S(1)}, f32[8,128]{1,0:T(8,128)S(1)}, f32[16,128]{1,0:T(8,128)S(1)}) custom-call(f32[16,128]{1,0:T(8,128)S(1)} %add.8.refs_0_, f32[16,128]{1,0:T(8,128)S(1)} %collective-permute-done.8.refs_1_, f32[16,128]{1,0:T(8,128)S(1)} %collective-permute-done.9.refs_2_, ...), custom_call_target="tpu_custom_call" | custom-call | flops 16777216 | tf_op jit(solution)/shard_map/step1/pallas_call | solution.py:28
  30.9 1.2 collective-permute-done.11.b
  32.0 0.6 collective-permute-start.14
  32.6 2.4 %collective-permute-start.13 = (f32[16,128]{1,0:T(8,128)S(1)}, f32[16,128]{1,0:T(8,128)S(1)}, u32[]{:S(2)}, u32[]{:S(2)}) collective-permute-start(f32[16,128]{1,0:T(8,128)S(1)} %add.9.refs_0_), channel_id=1, source_target_pairs={{0,2},{1,3},{2,0},{3,1},{4,6},{5,7},{6,4},{7,5},{8,10},{9,11},{10,... | collective-permute-start | bytes 24584 | tf_op jit(solution)/shard_map/ppermute | solution.py:324
  35.1 0.8 collective-permute-start.12
  36.0 1.5 %collective-permute-done.14.refs_3_ = f32[16,128]{1,0:T(8,128)S(1)} collective-permute-done((f32[16,128]{1,0:T(8,128)S(1)}, f32[16,128]{1,0:T(8,128)S(1)}, u32[]{:S(2)}, u32[]{:S(2)}) %collective-permute-start.14) | collective-permute-done | bytes 8224 | tf_op jit(solution)/shard_map/ppermute | solution.py:324
  37.5 1.2 collective-permute-done.12.refs_1_
  38.7 4.5 %step2.1 = (f32[64,128]{1,0:T(8,128)S(1)}, f32[64,128]{1,0:T(8,128)S(1)}, f32[8,128]{1,0:T(8,128)S(1)}, f32[16,128]{1,0:T(8,128)S(1)}) custom-call(f32[16,128]{1,0:T(8,128)S(1)} %add.9.refs_0_, f32[16,128]{1,0:T(8,128)S(1)} %collective-permute-done.12.refs_1_, f32[16,128]{1,0:T(8,128)S(1)} %collective-permute-done.13.refs_2_, ...), custom_call_target="tpu_custom_call" | custom-call | flops 16777216 | tf_op jit(solution)/shard_map/step2/pallas_call | solution.py:28
  43.3 1.2 collective-permute-done.15.b
  44.4 1.3 %collective-permute-start.18 = (f32[16,128]{1,0:T(8,128)S(1)}, f32[16,128]{1,0:T(8,128)S(1)}, u32[]{:S(2)}, u32[]{:S(2)}) collective-permute-start(f32[16,128]{1,0:T(8,128)S(1)} %add.10.refs_0_), channel_id=1, source_target_pairs={{0,1},{1,2},{2,3},{3,0},{4,5},{5,6},{6,7},{7,4},{8,9},{9,10},{10,1... | collective-permute-start | bytes 24584 | tf_op jit(solution)/shard_map/ppermute | solution.py:324
  45.8 1.8 %collective-permute-start.17 = (f32[16,128]{1,0:T(8,128)S(1)}, f32[16,128]{1,0:T(8,128)S(1)}, u32[]{:S(2)}, u32[]{:S(2)}) collective-permute-start(f32[16,128]{1,0:T(8,128)S(1)} %add.10.refs_0_), channel_id=1, source_target_pairs={{0,2},{1,3},{2,0},{3,1},{4,6},{5,7},{6,4},{7,5},{8,10},{9,11},{10,... | collective-permute-start | bytes 24584 | tf_op jit(solution)/shard_map/ppermute | solution.py:324
  47.6 0.7 collective-permute-start.16
  48.4 1.6 %collective-permute-done.18.refs_3_ = f32[16,128]{1,0:T(8,128)S(1)} collective-permute-done((f32[16,128]{1,0:T(8,128)S(1)}, f32[16,128]{1,0:T(8,128)S(1)}, u32[]{:S(2)}, u32[]{:S(2)}) %collective-permute-start.18) | collective-permute-done | bytes 8224 | tf_op jit(solution)/shard_map/ppermute | solution.py:324
  50.3 0.9 collective-permute-done.16.refs_1_
  51.2 4.5 %step3.1 = (f32[64,128]{1,0:T(8,128)S(1)}, f32[64,128]{1,0:T(8,128)S(1)}, f32[8,128]{1,0:T(8,128)S(1)}, f32[16,128]{1,0:T(8,128)S(1)}) custom-call(f32[16,128]{1,0:T(8,128)S(1)} %add.10.refs_0_, f32[16,128]{1,0:T(8,128)S(1)} %collective-permute-done.16.refs_1_, f32[16,128]{1,0:T(8,128)S(1)} %collective-permute-done.17.refs_2_, ...), custom_call_target="tpu_custom_call" | custom-call | flops 16777216 | tf_op jit(solution)/shard_map/step3/pallas_call | solution.py:28
  55.8 1.2 collective-permute-done.19.b
  57.0 1.2 collective-permute-start.22
  58.2 1.8 %collective-permute-start.21 = (f32[16,128]{1,0:T(8,128)S(1)}, f32[16,128]{1,0:T(8,128)S(1)}, u32[]{:S(2)}, u32[]{:S(2)}) collective-permute-start(f32[16,128]{1,0:T(8,128)S(1)} %add.11.refs_0_), channel_id=1, source_target_pairs={{0,2},{1,3},{2,0},{3,1},{4,6},{5,7},{6,4},{7,5},{8,10},{9,11},{10,... | collective-permute-start | bytes 24584 | tf_op jit(solution)/shard_map/ppermute | solution.py:324
  60.0 1.0 collective-permute-start.20
  61.1 1.3 %collective-permute-done.22.refs_3_ = f32[16,128]{1,0:T(8,128)S(1)} collective-permute-done((f32[16,128]{1,0:T(8,128)S(1)}, f32[16,128]{1,0:T(8,128)S(1)}, u32[]{:S(2)}, u32[]{:S(2)}) %collective-permute-start.22) | collective-permute-done | bytes 8224 | tf_op jit(solution)/shard_map/ppermute | solution.py:324
  62.8 0.9 collective-permute-done.20.refs_1_
  63.7 4.5 %step4.1 = (f32[64,128]{1,0:T(8,128)S(1)}, f32[64,128]{1,0:T(8,128)S(1)}, f32[8,128]{1,0:T(8,128)S(1)}, f32[16,128]{1,0:T(8,128)S(1)}) custom-call(f32[16,128]{1,0:T(8,128)S(1)} %add.11.refs_0_, f32[16,128]{1,0:T(8,128)S(1)} %collective-permute-done.20.refs_1_, f32[16,128]{1,0:T(8,128)S(1)} %collective-permute-done.21.refs_2_, ...), custom_call_target="tpu_custom_call" | custom-call | flops 16777216 | tf_op jit(solution)/shard_map/step4/pallas_call | solution.py:28
  68.2 1.2 collective-permute-done.23.b
  69.4 1.3 %collective-permute-start.26 = (f32[16,128]{1,0:T(8,128)S(1)}, f32[16,128]{1,0:T(8,128)S(1)}, u32[]{:S(2)}, u32[]{:S(2)}) collective-permute-start(f32[16,128]{1,0:T(8,128)S(1)} %add.12.refs_0_), channel_id=1, source_target_pairs={{0,1},{1,2},{2,3},{3,0},{4,5},{5,6},{6,7},{7,4},{8,9},{9,10},{10,1... | collective-permute-start | bytes 24584 | tf_op jit(solution)/shard_map/ppermute | solution.py:324
  70.7 2.0 %collective-permute-start.25 = (f32[16,128]{1,0:T(8,128)S(1)}, f32[16,128]{1,0:T(8,128)S(1)}, u32[]{:S(2)}, u32[]{:S(2)}) collective-permute-start(f32[16,128]{1,0:T(8,128)S(1)} %add.12.refs_0_), channel_id=1, source_target_pairs={{0,2},{1,3},{2,0},{3,1},{4,6},{5,7},{6,4},{7,5},{8,10},{9,11},{10,... | collective-permute-start | bytes 24584 | tf_op jit(solution)/shard_map/ppermute | solution.py:324
  72.7 0.7 collective-permute-start.24
  73.6 1.3 collective-permute-done.26.refs_3_
  75.3 1.1 collective-permute-done.24.refs_1_
  76.4 4.5 %step5.1 = (f32[64,128]{1,0:T(8,128)S(1)}, f32[64,128]{1,0:T(8,128)S(1)}, f32[8,128]{1,0:T(8,128)S(1)}, f32[16,128]{1,0:T(8,128)S(1)}) custom-call(f32[16,128]{1,0:T(8,128)S(1)} %add.12.refs_0_, f32[16,128]{1,0:T(8,128)S(1)} %collective-permute-done.24.refs_1_, f32[16,128]{1,0:T(8,128)S(1)} %collective-permute-done.25.refs_2_, ...), custom_call_target="tpu_custom_call" | custom-call | flops 16777216 | tf_op jit(solution)/shard_map/step5/pallas_call | solution.py:28
  81.0 1.2 collective-permute-done.27.b
  82.1 1.0 collective-permute-start.30
  83.1 2.0 %collective-permute-start.29 = (f32[16,128]{1,0:T(8,128)S(1)}, f32[16,128]{1,0:T(8,128)S(1)}, u32[]{:S(2)}, u32[]{:S(2)}) collective-permute-start(f32[16,128]{1,0:T(8,128)S(1)} %add.13.refs_0_), channel_id=1, source_target_pairs={{0,2},{1,3},{2,0},{3,1},{4,6},{5,7},{6,4},{7,5},{8,10},{9,11},{10,... | collective-permute-start | bytes 24584 | tf_op jit(solution)/shard_map/ppermute | solution.py:324
  85.2 0.8 collective-permute-start.28
  86.1 1.5 %collective-permute-done.30.refs_3_ = f32[16,128]{1,0:T(8,128)S(1)} collective-permute-done((f32[16,128]{1,0:T(8,128)S(1)}, f32[16,128]{1,0:T(8,128)S(1)}, u32[]{:S(2)}, u32[]{:S(2)}) %collective-permute-start.30) | collective-permute-done | bytes 8224 | tf_op jit(solution)/shard_map/ppermute | solution.py:324
  87.7 1.1 collective-permute-done.28.refs_1_
  88.8 4.5 %step6.1 = (f32[64,128]{1,0:T(8,128)S(1)}, f32[64,128]{1,0:T(8,128)S(1)}, f32[8,128]{1,0:T(8,128)S(1)}, f32[16,128]{1,0:T(8,128)S(1)}) custom-call(f32[16,128]{1,0:T(8,128)S(1)} %add.13.refs_0_, f32[16,128]{1,0:T(8,128)S(1)} %collective-permute-done.28.refs_1_, f32[16,128]{1,0:T(8,128)S(1)} %collective-permute-done.29.refs_2_, ...), custom_call_target="tpu_custom_call" | custom-call | flops 16777216 | tf_op jit(solution)/shard_map/step6/pallas_call | solution.py:28
  93.4 1.2 collective-permute-done.31.b
  94.5 1.3 %collective-permute-start.34 = (f32[16,128]{1,0:T(8,128)S(1)}, f32[16,128]{1,0:T(8,128)S(1)}, u32[]{:S(2)}, u32[]{:S(2)}) collective-permute-start(f32[16,128]{1,0:T(8,128)S(1)} %add.14.refs_0_), channel_id=1, source_target_pairs={{0,1},{1,2},{2,3},{3,0},{4,5},{5,6},{6,7},{7,4},{8,9},{9,10},{10,1... | collective-permute-start | bytes 24584 | tf_op jit(solution)/shard_map/ppermute | solution.py:324
  95.9 1.8 %collective-permute-start.33 = (f32[16,128]{1,0:T(8,128)S(1)}, f32[16,128]{1,0:T(8,128)S(1)}, u32[]{:S(2)}, u32[]{:S(2)}) collective-permute-start(f32[16,128]{1,0:T(8,128)S(1)} %add.14.refs_0_), channel_id=1, source_target_pairs={{0,2},{1,3},{2,0},{3,1},{4,6},{5,7},{6,4},{7,5},{8,10},{9,11},{10,... | collective-permute-start | bytes 24584 | tf_op jit(solution)/shard_map/ppermute | solution.py:324
  97.7 0.7 collective-permute-start.32
  98.5 1.5 %collective-permute-done.34.refs_3_ = f32[16,128]{1,0:T(8,128)S(1)} collective-permute-done((f32[16,128]{1,0:T(8,128)S(1)}, f32[16,128]{1,0:T(8,128)S(1)}, u32[]{:S(2)}, u32[]{:S(2)}) %collective-permute-start.34) | collective-permute-done | bytes 8224 | tf_op jit(solution)/shard_map/ppermute | solution.py:324
  100.4 0.9 collective-permute-done.32.refs_1_
  101.3 4.5 %step7.1 = (f32[64,128]{1,0:T(8,128)S(1)}, f32[64,128]{1,0:T(8,128)S(1)}, f32[8,128]{1,0:T(8,128)S(1)}, f32[16,128]{1,0:T(8,128)S(1)}) custom-call(f32[16,128]{1,0:T(8,128)S(1)} %add.14.refs_0_, f32[16,128]{1,0:T(8,128)S(1)} %collective-permute-done.32.refs_1_, f32[16,128]{1,0:T(8,128)S(1)} %collective-permute-done.33.refs_2_, ...), custom_call_target="tpu_custom_call" | custom-call | flops 16777216 | tf_op jit(solution)/shard_map/step7/pallas_call | solution.py:28
  105.9 1.2 collective-permute-done.35.b
  107.1 1.2 collective-permute-start.38
  108.3 1.8 %collective-permute-start.37 = (f32[16,128]{1,0:T(8,128)S(1)}, f32[16,128]{1,0:T(8,128)S(1)}, u32[]{:S(2)}, u32[]{:S(2)}) collective-permute-start(f32[16,128]{1,0:T(8,128)S(1)} %add.15.refs_0_), channel_id=1, source_target_pairs={{0,2},{1,3},{2,0},{3,1},{4,6},{5,7},{6,4},{7,5},{8,10},{9,11},{10,... | collective-permute-start | bytes 24584 | tf_op jit(solution)/shard_map/ppermute | solution.py:324
  110.1 1.0 collective-permute-start.36
  111.2 1.3 %collective-permute-done.38.refs_3_ = f32[16,128]{1,0:T(8,128)S(1)} collective-permute-done((f32[16,128]{1,0:T(8,128)S(1)}, f32[16,128]{1,0:T(8,128)S(1)}, u32[]{:S(2)}, u32[]{:S(2)}) %collective-permute-start.38) | collective-permute-done | bytes 8224 | tf_op jit(solution)/shard_map/ppermute | solution.py:324
  112.9 0.9 collective-permute-done.36.refs_1_
  113.8 12.2 %last.1 = f32[2048,4096]{1,0:T(8,128)} custom-call(f32[16,128]{1,0:T(8,128)S(1)} %add.15.refs_0_, f32[16,128]{1,0:T(8,128)S(1)} %collective-permute-done.36.refs_1_, f32[16,128]{1,0:T(8,128)S(1)} %collective-permute-done.37.refs_2_, f32[16,128]{1,0:T(8,128)S(1)} %collective-permute-done.38.refs_3_, f32[64,128]{1,0:T(8,128)S(1)} %get-tuple-element.49.refs_5_.refs_0_.refs_4_, ...), custom_call_target="tpu_custom_call" | custom-call | flops 268435456 | bytes 67108864 | tf_op jit(solution)/shard_map/last/pallas_call | solution.py:402
  (42 shorter events, 5.2 us)
Async XLA Ops:
  0.0 13.4 %copy-start = (f32[1,2048,4096]{2,1,0:T(8,128)S(1)}, f32[1,2048,4096]{2,1,0:T(8,128)}, u32[]{:S(2)}) copy-start(f32[1,2048,4096]{2,1,0:T(8,128)} %param.1) | copy-start | bytes 100663296
  1.7 7.6 %collective-permute-start.2 = (f32[128,128]{1,0:T(8,128)S(1)}, f32[128,128]{1,0:T(8,128)S(1)}, u32[]{:S(2)}, u32[]{:S(2)}) collective-permute-start(f32[128,128]{1,0:T(8,128)S(1)} %panel.1.refs_0_), channel_id=1, source_target_pairs={{0,1},{1,2},{2,3},{3,0},{4,5},{5,6},{6,7},{7,4},{8,9},{9,10},{10,1... | collective-permute-start | bytes 196616 | tf_op jit(solution)/shard_map/ppermute | solution.py:324
  4.8 7.1 %collective-permute-start.1 = (f32[128,128]{1,0:T(8,128)S(1)}, f32[128,128]{1,0:T(8,128)S(1)}, u32[]{:S(2)}, u32[]{:S(2)}) collective-permute-start(f32[128,128]{1,0:T(8,128)S(1)} %panel.1.refs_0_), channel_id=1, source_target_pairs={{0,2},{1,3},{2,0},{3,1},{4,6},{5,7},{6,4},{7,5},{8,10},{9,11},{10,... | collective-permute-start | bytes 196616 | tf_op jit(solution)/shard_map/ppermute | solution.py:324
  7.4 4.7 %collective-permute-start = (f32[128,128]{1,0:T(8,128)S(1)}, f32[128,128]{1,0:T(8,128)S(1)}, u32[]{:S(2)}, u32[]{:S(2)}) collective-permute-start(f32[128,128]{1,0:T(8,128)S(1)} %panel.1.refs_0_), channel_id=1, source_target_pairs={{0,3},{1,0},{2,1},{3,2},{4,7},{5,4},{6,5},{7,6},{8,11},{9,8},{10,9... | collective-permute-start | bytes 196616 | tf_op jit(solution)/shard_map/ppermute | solution.py:324
  8.7 3.7 %collective-permute-start.3 = (f32[128,128]{1,0:T(8,128)S(1)}, f32[128,128]{1,0:T(8,128)S(1)}, u32[]{:S(2)}, u32[]{:S(2)}) collective-permute-start(f32[128,128]{1,0:T(8,128)S(1)} %panel.1.refs_0_), channel_id=1, source_target_pairs={{0,4},{4,0},{1,5},{5,1},{2,6},{6,2},{3,7},{7,3},{8,12},{12,8},{9,1... | collective-permute-start | bytes 196616 | tf_op jit(solution)/shard_map/ppermute | solution.py:328
  9.3 3.1 %collective-permute-start.6 = (f32[128,128]{1,0:T(8,128)S(1)}, f32[128,128]{1,0:T(8,128)S(1)}, u32[]{:S(2)}, u32[]{:S(2)}) collective-permute-start(f32[128,128]{1,0:T(8,128)S(1)} %collective-permute-done.2.refs_3_), channel_id=1, source_target_pairs={{0,4},{4,0},{1,5},{5,1},{2,6},{6,2},{3,7},{7,3},{8,12},{12,8},{9,1... | collective-permute-start | bytes 196616 | tf_op jit(solution)/shard_map/ppermute | solution.py:328
  11.9 1.3 collective-permute-start.5
  12.1 1.3 collective-permute-start.4
  17.6 1.2 collective-permute-start.7
  18.9 5.4 %collective-permute-start.10 = (f32[16,128]{1,0:T(8,128)S(1)}, f32[16,128]{1,0:T(8,128)S(1)}, u32[]{:S(2)}, u32[]{:S(2)}) collective-permute-start(f32[16,128]{1,0:T(8,128)S(1)} %add.8.refs_0_), channel_id=1, source_target_pairs={{0,1},{1,2},{2,3},{3,0},{4,5},{5,6},{6,7},{7,4},{8,9},{9,10},{10,1... | collective-permute-start | bytes 24584 | tf_op jit(solution)/shard_map/ppermute | solution.py:324
  20.5 4.6 %collective-permute-start.9 = (f32[16,128]{1,0:T(8,128)S(1)}, f32[16,128]{1,0:T(8,128)S(1)}, u32[]{:S(2)}, u32[]{:S(2)}) collective-permute-start(f32[16,128]{1,0:T(8,128)S(1)} %add.8.refs_0_), channel_id=1, source_target_pairs={{0,2},{1,3},{2,0},{3,1},{4,6},{5,7},{6,4},{7,5},{8,10},{9,11},{10,... | collective-permute-start | bytes 24584 | tf_op jit(solution)/shard_map/ppermute | solution.py:324
  22.6 3.7 %collective-permute-start.8 = (f32[16,128]{1,0:T(8,128)S(1)}, f32[16,128]{1,0:T(8,128)S(1)}, u32[]{:S(2)}, u32[]{:S(2)}) collective-permute-start(f32[16,128]{1,0:T(8,128)S(1)} %add.8.refs_0_), channel_id=1, source_target_pairs={{0,3},{1,0},{2,1},{3,2},{4,7},{5,4},{6,5},{7,6},{8,11},{9,8},{10,9... | collective-permute-start | bytes 24584 | tf_op jit(solution)/shard_map/ppermute | solution.py:324
  30.8 1.2 collective-permute-start.11
  32.0 5.4 %collective-permute-start.14 = (f32[16,128]{1,0:T(8,128)S(1)}, f32[16,128]{1,0:T(8,128)S(1)}, u32[]{:S(2)}, u32[]{:S(2)}) collective-permute-start(f32[16,128]{1,0:T(8,128)S(1)} %add.9.refs_0_), channel_id=1, source_target_pairs={{0,1},{1,2},{2,3},{3,0},{4,5},{5,6},{6,7},{7,4},{8,9},{9,10},{10,1... | collective-permute-start | bytes 24584 | tf_op jit(solution)/shard_map/ppermute | solution.py:324
  32.6 4.8 %collective-permute-start.13 = (f32[16,128]{1,0:T(8,128)S(1)}, f32[16,128]{1,0:T(8,128)S(1)}, u32[]{:S(2)}, u32[]{:S(2)}) collective-permute-start(f32[16,128]{1,0:T(8,128)S(1)} %add.9.refs_0_), channel_id=1, source_target_pairs={{0,2},{1,3},{2,0},{3,1},{4,6},{5,7},{6,4},{7,5},{8,10},{9,11},{10,... | collective-permute-start | bytes 24584 | tf_op jit(solution)/shard_map/ppermute | solution.py:324
  35.1 3.7 %collective-permute-start.12 = (f32[16,128]{1,0:T(8,128)S(1)}, f32[16,128]{1,0:T(8,128)S(1)}, u32[]{:S(2)}, u32[]{:S(2)}) collective-permute-start(f32[16,128]{1,0:T(8,128)S(1)} %add.9.refs_0_), channel_id=1, source_target_pairs={{0,3},{1,0},{2,1},{3,2},{4,7},{5,4},{6,5},{7,6},{8,11},{9,8},{10,9... | collective-permute-start | bytes 24584 | tf_op jit(solution)/shard_map/ppermute | solution.py:324
  43.2 1.2 collective-permute-start.15
  44.4 5.5 %collective-permute-start.18 = (f32[16,128]{1,0:T(8,128)S(1)}, f32[16,128]{1,0:T(8,128)S(1)}, u32[]{:S(2)}, u32[]{:S(2)}) collective-permute-start(f32[16,128]{1,0:T(8,128)S(1)} %add.10.refs_0_), channel_id=1, source_target_pairs={{0,1},{1,2},{2,3},{3,0},{4,5},{5,6},{6,7},{7,4},{8,9},{9,10},{10,1... | collective-permute-start | bytes 24584 | tf_op jit(solution)/shard_map/ppermute | solution.py:324
  45.8 4.5 %collective-permute-start.17 = (f32[16,128]{1,0:T(8,128)S(1)}, f32[16,128]{1,0:T(8,128)S(1)}, u32[]{:S(2)}, u32[]{:S(2)}) collective-permute-start(f32[16,128]{1,0:T(8,128)S(1)} %add.10.refs_0_), channel_id=1, source_target_pairs={{0,2},{1,3},{2,0},{3,1},{4,6},{5,7},{6,4},{7,5},{8,10},{9,11},{10,... | collective-permute-start | bytes 24584 | tf_op jit(solution)/shard_map/ppermute | solution.py:324
  47.6 3.7 %collective-permute-start.16 = (f32[16,128]{1,0:T(8,128)S(1)}, f32[16,128]{1,0:T(8,128)S(1)}, u32[]{:S(2)}, u32[]{:S(2)}) collective-permute-start(f32[16,128]{1,0:T(8,128)S(1)} %add.10.refs_0_), channel_id=1, source_target_pairs={{0,3},{1,0},{2,1},{3,2},{4,7},{5,4},{6,5},{7,6},{8,11},{9,8},{10,9... | collective-permute-start | bytes 24584 | tf_op jit(solution)/shard_map/ppermute | solution.py:324
  55.7 1.2 collective-permute-start.19
  57.0 5.4 %collective-permute-start.22 = (f32[16,128]{1,0:T(8,128)S(1)}, f32[16,128]{1,0:T(8,128)S(1)}, u32[]{:S(2)}, u32[]{:S(2)}) collective-permute-start(f32[16,128]{1,0:T(8,128)S(1)} %add.11.refs_0_), channel_id=1, source_target_pairs={{0,1},{1,2},{2,3},{3,0},{4,5},{5,6},{6,7},{7,4},{8,9},{9,10},{10,1... | collective-permute-start | bytes 24584 | tf_op jit(solution)/shard_map/ppermute | solution.py:324
  58.2 4.5 %collective-permute-start.21 = (f32[16,128]{1,0:T(8,128)S(1)}, f32[16,128]{1,0:T(8,128)S(1)}, u32[]{:S(2)}, u32[]{:S(2)}) collective-permute-start(f32[16,128]{1,0:T(8,128)S(1)} %add.11.refs_0_), channel_id=1, source_target_pairs={{0,2},{1,3},{2,0},{3,1},{4,6},{5,7},{6,4},{7,5},{8,10},{9,11},{10,... | collective-permute-start | bytes 24584 | tf_op jit(solution)/shard_map/ppermute | solution.py:324
  60.0 3.7 %collective-permute-start.20 = (f32[16,128]{1,0:T(8,128)S(1)}, f32[16,128]{1,0:T(8,128)S(1)}, u32[]{:S(2)}, u32[]{:S(2)}) collective-permute-start(f32[16,128]{1,0:T(8,128)S(1)} %add.11.refs_0_), channel_id=1, source_target_pairs={{0,3},{1,0},{2,1},{3,2},{4,7},{5,4},{6,5},{7,6},{8,11},{9,8},{10,9... | collective-permute-start | bytes 24584 | tf_op jit(solution)/shard_map/ppermute | solution.py:324
  68.1 1.2 collective-permute-start.23
  69.4 5.4 %collective-permute-start.26 = (f32[16,128]{1,0:T(8,128)S(1)}, f32[16,128]{1,0:T(8,128)S(1)}, u32[]{:S(2)}, u32[]{:S(2)}) collective-permute-start(f32[16,128]{1,0:T(8,128)S(1)} %add.12.refs_0_), channel_id=1, source_target_pairs={{0,1},{1,2},{2,3},{3,0},{4,5},{5,6},{6,7},{7,4},{8,9},{9,10},{10,1... | collective-permute-start | bytes 24584 | tf_op jit(solution)/shard_map/ppermute | solution.py:324
  70.7 4.5 %collective-permute-start.25 = (f32[16,128]{1,0:T(8,128)S(1)}, f32[16,128]{1,0:T(8,128)S(1)}, u32[]{:S(2)}, u32[]{:S(2)}) collective-permute-start(f32[16,128]{1,0:T(8,128)S(1)} %add.12.refs_0_), channel_id=1, source_target_pairs={{0,2},{1,3},{2,0},{3,1},{4,6},{5,7},{6,4},{7,5},{8,10},{9,11},{10,... | collective-permute-start | bytes 24584 | tf_op jit(solution)/shard_map/ppermute | solution.py:324
  72.7 3.7 %collective-permute-start.24 = (f32[16,128]{1,0:T(8,128)S(1)}, f32[16,128]{1,0:T(8,128)S(1)}, u32[]{:S(2)}, u32[]{:S(2)}) collective-permute-start(f32[16,128]{1,0:T(8,128)S(1)} %add.12.refs_0_), channel_id=1, source_target_pairs={{0,3},{1,0},{2,1},{3,2},{4,7},{5,4},{6,5},{7,6},{8,11},{9,8},{10,9... | collective-permute-start | bytes 24584 | tf_op jit(solution)/shard_map/ppermute | solution.py:324
  80.9 1.2 collective-permute-start.27
  82.1 5.4 %collective-permute-start.30 = (f32[16,128]{1,0:T(8,128)S(1)}, f32[16,128]{1,0:T(8,128)S(1)}, u32[]{:S(2)}, u32[]{:S(2)}) collective-permute-start(f32[16,128]{1,0:T(8,128)S(1)} %add.13.refs_0_), channel_id=1, source_target_pairs={{0,1},{1,2},{2,3},{3,0},{4,5},{5,6},{6,7},{7,4},{8,9},{9,10},{10,1... | collective-permute-start | bytes 24584 | tf_op jit(solution)/shard_map/ppermute | solution.py:324
  83.1 4.6 %collective-permute-start.29 = (f32[16,128]{1,0:T(8,128)S(1)}, f32[16,128]{1,0:T(8,128)S(1)}, u32[]{:S(2)}, u32[]{:S(2)}) collective-permute-start(f32[16,128]{1,0:T(8,128)S(1)} %add.13.refs_0_), channel_id=1, source_target_pairs={{0,2},{1,3},{2,0},{3,1},{4,6},{5,7},{6,4},{7,5},{8,10},{9,11},{10,... | collective-permute-start | bytes 24584 | tf_op jit(solution)/shard_map/ppermute | solution.py:324
  85.2 3.7 %collective-permute-start.28 = (f32[16,128]{1,0:T(8,128)S(1)}, f32[16,128]{1,0:T(8,128)S(1)}, u32[]{:S(2)}, u32[]{:S(2)}) collective-permute-start(f32[16,128]{1,0:T(8,128)S(1)} %add.13.refs_0_), channel_id=1, source_target_pairs={{0,3},{1,0},{2,1},{3,2},{4,7},{5,4},{6,5},{7,6},{8,11},{9,8},{10,9... | collective-permute-start | bytes 24584 | tf_op jit(solution)/shard_map/ppermute | solution.py:324
  93.3 1.2 collective-permute-start.31
  94.5 5.5 %collective-permute-start.34 = (f32[16,128]{1,0:T(8,128)S(1)}, f32[16,128]{1,0:T(8,128)S(1)}, u32[]{:S(2)}, u32[]{:S(2)}) collective-permute-start(f32[16,128]{1,0:T(8,128)S(1)} %add.14.refs_0_), channel_id=1, source_target_pairs={{0,1},{1,2},{2,3},{3,0},{4,5},{5,6},{6,7},{7,4},{8,9},{9,10},{10,1... | collective-permute-start | bytes 24584 | tf_op jit(solution)/shard_map/ppermute | solution.py:324
  95.9 4.5 %collective-permute-start.33 = (f32[16,128]{1,0:T(8,128)S(1)}, f32[16,128]{1,0:T(8,128)S(1)}, u32[]{:S(2)}, u32[]{:S(2)}) collective-permute-start(f32[16,128]{1,0:T(8,128)S(1)} %add.14.refs_0_), channel_id=1, source_target_pairs={{0,2},{1,3},{2,0},{3,1},{4,6},{5,7},{6,4},{7,5},{8,10},{9,11},{10,... | collective-permute-start | bytes 24584 | tf_op jit(solution)/shard_map/ppermute | solution.py:324
  97.7 3.7 %collective-permute-start.32 = (f32[16,128]{1,0:T(8,128)S(1)}, f32[16,128]{1,0:T(8,128)S(1)}, u32[]{:S(2)}, u32[]{:S(2)}) collective-permute-start(f32[16,128]{1,0:T(8,128)S(1)} %add.14.refs_0_), channel_id=1, source_target_pairs={{0,3},{1,0},{2,1},{3,2},{4,7},{5,4},{6,5},{7,6},{8,11},{9,8},{10,9... | collective-permute-start | bytes 24584 | tf_op jit(solution)/shard_map/ppermute | solution.py:324
  105.8 1.2 collective-permute-start.35
  107.1 5.4 %collective-permute-start.38 = (f32[16,128]{1,0:T(8,128)S(1)}, f32[16,128]{1,0:T(8,128)S(1)}, u32[]{:S(2)}, u32[]{:S(2)}) collective-permute-start(f32[16,128]{1,0:T(8,128)S(1)} %add.15.refs_0_), channel_id=1, source_target_pairs={{0,1},{1,2},{2,3},{3,0},{4,5},{5,6},{6,7},{7,4},{8,9},{9,10},{10,1... | collective-permute-start | bytes 24584 | tf_op jit(solution)/shard_map/ppermute | solution.py:324
  108.3 4.5 %collective-permute-start.37 = (f32[16,128]{1,0:T(8,128)S(1)}, f32[16,128]{1,0:T(8,128)S(1)}, u32[]{:S(2)}, u32[]{:S(2)}) collective-permute-start(f32[16,128]{1,0:T(8,128)S(1)} %add.15.refs_0_), channel_id=1, source_target_pairs={{0,2},{1,3},{2,0},{3,1},{4,6},{5,7},{6,4},{7,5},{8,10},{9,11},{10,... | collective-permute-start | bytes 24584 | tf_op jit(solution)/shard_map/ppermute | solution.py:324
  110.1 3.7 %collective-permute-start.36 = (f32[16,128]{1,0:T(8,128)S(1)}, f32[16,128]{1,0:T(8,128)S(1)}, u32[]{:S(2)}, u32[]{:S(2)}) collective-permute-start(f32[16,128]{1,0:T(8,128)S(1)} %add.15.refs_0_), channel_id=1, source_target_pairs={{0,3},{1,0},{2,1},{3,2},{4,7},{5,4},{6,5},{7,6},{8,11},{9,8},{10,9... | collective-permute-start | bytes 24584 | tf_op jit(solution)/shard_map/ppermute | solution.py:324

commit v2 on v1

--- a/solution.py
+++ b/solution.py
@@ -41,34 +41,6 @@
     return jax.ShapeDtypeStruct(shape, f32)
 
 
-def load_body(src, dst, sems, *, pieces):
-    rows = src.shape[0] // pieces
-    copies = []
-    for k in range(pieces):
-        part = pl.ds(k * rows, rows)
-        copies.append(pltpu.make_async_copy(src.at[part], dst.at[part], sems.at[k]))
-    for copy in copies:
-        copy.start()
-    for copy in copies:
-        copy.wait()
-
-
-def load(block):
-    pieces = 8
-    return pl.pallas_call(
-        functools.partial(load_body, pieces=pieces),
-        out_shape=VMEM(block.shape, f32),
-        in_specs=[pl.BlockSpec(memory_space=pl.ANY)],
-        out_specs=pl.BlockSpec(memory_space=VMEM),
-        scratch_shapes=[pltpu.SemaphoreType.DMA((pieces,))],
-        compiler_params=pltpu.CompilerParams(vmem_limit_bytes=15 * MIB),
-        cost_estimate=pl.CostEstimate(
-            flops=4 * 10**8, bytes_accessed=2 * block.size * 4, transcendentals=0
-        ),
-        name="load",
-    )(pltpu.with_memory_space_constraint(block, pltpu.HBM))
-
-
 def panel_body(src, dst, tall, sem, *, tiles):
     copy = pltpu.make_async_copy(src.at[:, pl.ds(0, LANES)], tall, sem)
     copy.start()
@@ -93,21 +65,32 @@
     )(pltpu.with_memory_space_constraint(block, pltpu.HBM))
 
 
-def gather_panel_body(*refs, count, sections, tiles):
-    dst = refs[-1]
+def pick_body(own, other, dst):
+    dst[...] = jnp.where(lax.axis_index("section") == 0, own[...], other[...])
+
+
+def gather_panel_body(*refs, tiles):
+    *pieces, dst = refs
+    total = tiles * len(pieces)
+    for piece, place in zip(pieces, ranges_of(len(pieces))):
+        for column in range(NB):
+            part = pl.multiple_of(column * total + place * tiles, SUBLANES)
+            dst[pl.ds(part, tiles), :] = piece[pl.ds(column * tiles, tiles), :]
+
+
+def ranges_of(count):
     row = lax.axis_index("row")
-    section = lax.axis_index("section")
-    own = refs[:count]
-    other = refs[count:-1]
-    total = tiles * count
-    for k in range(count):
-        place = lax.rem(row + k, count) * tiles
-        for column in range(NB):
-            part = pl.ds(column * tiles, tiles)
-            value = own[k][part, :]
-            if sections == 2:
-                value = jnp.where(section == 0, value, other[k][part, :])
-            dst[pl.ds(pl.multiple_of(column * total + place, SUBLANES), tiles), :] = value
+    if count == 1:
+        return [row * 0]
+    upper = lax.axis_index("section") == 1
+    far = jnp.bitwise_xor(row, 3)
+    middle = jnp.bitwise_xor(row, 2)
+    return [
+        row,
+        jnp.bitwise_xor(row, 1),
+        jnp.where(upper, far, middle),
+        jnp.where(upper, middle, far),
+    ]
 
 
 def total_of(value):
@@ -142,11 +125,10 @@
         turned = wide[...].T
         part[pl.ds(t, 1), :] = jnp.sum(turned, axis=0, keepdims=True)
 
+    wide[...] = jnp.zeros_like(wide)
+
     def step(t, carry):
-        @pl.when(t > 0)
-        def _():
-            turn(t - 1)
-
+        turn(jnp.maximum(t - 1, 0))
         for g in range(LANES // SUBLANES):
             rows = pl.ds(pl.multiple_of(t * LANES + g * SUBLANES, SUBLANES), SUBLANES)
             sums = [None, None]
@@ -170,11 +152,9 @@
 
 
 def finish_image(pieces, offset, reflector, facts, image_ref):
-    count = len(pieces)
-    row = lax.axis_index("row")
-    for k, piece in enumerate(pieces):
+    for piece, place in zip(pieces, ranges_of(len(pieces))):
         tiles = piece.shape[0]
-        place = lax.rem(row + k, count) * tiles
+        place = place * tiles
         image_ref[pl.ds(pl.multiple_of(place, SUBLANES), tiles), :] = piece[...]
     image = image_ref[...]
     if offset is not None:
@@ -305,27 +285,24 @@
         copy_out(t, t % slots).wait()
 
 
-def turn_by(axis, size, shift):
-    return [(i, (i + shift) % size) for i in range(size)]
-
-
 def local(matrices):
     height, breadth = matrices.shape[1:]
     count = lax.axis_size("row")
     sections = lax.axis_size("section")
     total = count * height // LANES
     tiles = height // LANES
-    direct = count <= 4 and sections == 2
+    direct = count == 4 and sections == 2
     block = matrices.reshape(height, breadth)
-
-    def rows_of(value):
-        got = {}
-        for k in range(1, count):
-            got[k] = lax.ppermute(value, "row", turn_by("row", count, count - k))
-        return [value] + [got[k] for k in range(1, count)]
 
     def swap(value):
         return lax.ppermute(value, "section", [(0, 1), (1, 0)])
+
+    def rows_of(value):
+        near = lax.ppermute(value, "row", [(r, r ^ 1) for r in range(count)])
+        apart = [(r, r ^ 2) for r in range(count)]
+        apart += [(count + r, count + (r ^ 3)) for r in range(count)]
+        first = lax.ppermute(value, ("section", "row"), apart)
+        return [value, near, first, swap(first)]
 
     def exchange(part):
         if direct:
@@ -336,10 +313,9 @@
 
     own = panel(block)
     if direct:
-        kept = rows_of(own)
-        kept = kept + [swap(value) for value in kept]
-        body = functools.partial(gather_panel_body, count=count, sections=2, tiles=tiles)
-        columns = call(body, out(NB * total, LANES), kept, limit=2 * MIB, name="lay")
+        own = call(pick_body, out(*own.shape), [own, swap(own)], limit=2 * MIB, name="pick")
+        body = functools.partial(gather_panel_body, tiles=tiles)
+        columns = call(body, out(NB * total, LANES), rows_of(own), limit=2 * MIB, name="lay")
     else:
         own = jnp.where(lax.axis_index("section") == 0, own, 0.0)
         own = lax.psum(own, "section").reshape(NB, tiles, LANES)

time: 126 us -> 105 us (0.83)
  Pallas kernels: 50.4 us -> 39.1 us
  waiting for transfers between devices: 35.2 us -> 27.9 us
  starting transfers between devices: 40.1 us -> 37.9 us
    pallas_call x24 -> x25, Pallas kernels: 36.5 us -> 25.2 us  [call(): pl.pallas_call(body, out_shape=outs, in_specs=specs, out_specs=jax.tree.m...]
    ppermute x27 -> x18, waiting for transfers between devices: 25.3 us -> 18.6 us  [the longest x9 10.1 us: rows_of(): near = lax.ppermute(value, 'row', [(r, r ^ 1) for r in range(count)])]
    ppermute x27 -> x18, starting transfers between devices: 38.9 us -> 35.6 us  [the longest x9 20.9 us: rows_of(): first = lax.ppermute(value, ('section', 'row'), apart)]
    ppermute x12 -> x18, waiting for transfers between devices: 9.97 us -> 9.31 us  [swap(): return lax.ppermute(value, 'section', [(0, 1), (1, 0)])]
  transfers between devices with their start and end apart: 39 -> 36, of which waited for: 36 -> 29; matrix products, arithmetic and copies ran while one was open for 0% -> 0% of each run, Pallas kernels for 1% -> 1%
where the time goes in v2:
time: 105 us
  Pallas kernels  39.1 us (37%)
  starting transfers between devices  37.9 us (36%)
  waiting for transfers between devices  27.9 us (27%)
    pallas_call x25, Pallas kernels, call(): pl.pallas_call(body, out_shape=outs, in_specs=specs, out_specs=jax.tree.m...  25.2 us
    ppermute x9, starting transfers between devices, rows_of(): first = lax.ppermute(value, ('section', 'row'), apart)  20.9 us
    ppermute x9, starting transfers between devices, rows_of(): near = lax.ppermute(value, 'row', [(r, r ^ 1) for r in range(count)])  14.7 us
    pallas_call x1, Pallas kernels, local(): pl.pallas_call(functools.partial(last_body, count=len(pieces), breadth=br...  12.2 us
    ppermute x9, waiting for transfers between devices, rows_of(): near = lax.ppermute(value, 'row', [(r, r ^ 1) for r in range(count)])  10.1 us
    ppermute x18, waiting for transfers between devices, swap(): return lax.ppermute(value, 'section', [(0, 1), (1, 0)])  9.31 us
    ppermute x9, waiting for transfers between devices, rows_of(): first = lax.ppermute(value, ('section', 'row'), apart)  8.45 us
    ppermute x18, starting transfers between devices, swap(): return lax.ppermute(value, 'section', [(0, 1), (1, 0)])  2.34 us
  transfers between devices with their start and end apart: 36, of which 29 were waited for; matrix products, arithmetic and copies ran while one was open for 0% of the time, Pallas kernels for 1%

profile of v2, /device:TPU:0, one launch (start us, length us, event | category | flops | bytes accessed | tf_op | source)
XLA Modules:
  0.0 105.2 jit_solution(2594457119256924074)
XLA Ops:
  0.0 1.7 %panel.1.own = f32[128,128]{1,0:T(8,128)S(1)} custom-call(f32[2048,4096]{1,0:T(8,128)} %bitcast.2), custom_call_target="tpu_custom_call" | custom-call | flops 10000000 | bytes 2097152 | tf_op jit(solution)/shard_map/panel/pallas_call | solution.py:56
  1.7 0.6 collective-permute-start
  2.3 0.9 collective-permute-done.other
  3.2 4.0 %collective-permute-start.2 = (f32[128,128]{1,0:T(8,128)S(1)}, f32[128,128]{1,0:T(8,128)S(1)}, u32[]{:S(2)}, u32[]{:S(2)}) collective-permute-start(f32[128,128]{1,0:T(8,128)S(1)} %pick.1.refs_0_), channel_id=1, source_target_pairs={{0,2},{1,3},{2,0},{3,1},{4,7},{5,6},{6,5},{7,4},{8,10},{9,11},{10,... | collective-permute-start | bytes 196616 | tf_op jit(solution)/shard_map/ppermute | solution.py:304
  7.2 1.6 %collective-permute-start.1 = (f32[128,128]{1,0:T(8,128)S(1)}, f32[128,128]{1,0:T(8,128)S(1)}, u32[]{:S(2)}, u32[]{:S(2)}) collective-permute-start(f32[128,128]{1,0:T(8,128)S(1)} %pick.1.refs_0_), channel_id=1, source_target_pairs={{0,1},{1,0},{2,3},{3,2},{4,5},{5,4},{6,7},{7,6},{8,9},{9,8},{10,11... | collective-permute-start | bytes 196616 | tf_op jit(solution)/shard_map/ppermute | solution.py:301
  8.7 2.1 %collective-permute-done.2.refs_2_ = f32[128,128]{1,0:T(8,128)S(1)} collective-permute-done((f32[128,128]{1,0:T(8,128)S(1)}, f32[128,128]{1,0:T(8,128)S(1)}, u32[]{:S(2)}, u32[]{:S(2)}) %collective-permute-start.2) | collective-permute-done | bytes 65568 | tf_op jit(solution)/shard_map/ppermute | solution.py:304
  10.8 1.3 %collective-permute-done.1.refs_1_ = f32[128,128]{1,0:T(8,128)S(1)} collective-permute-done((f32[128,128]{1,0:T(8,128)S(1)}, f32[128,128]{1,0:T(8,128)S(1)}, u32[]{:S(2)}, u32[]{:S(2)}) %collective-permute-start.1) | collective-permute-done | bytes 65568 | tf_op jit(solution)/shard_map/ppermute | solution.py:301
  12.2 2.8 %first.1 = (f32[64,128]{1,0:T(8,128)S(1)}, f32[8,128]{1,0:T(8,128)S(1)}, f32[16,128]{1,0:T(8,128)S(1)}) custom-call(f32[512,128]{1,0:T(8,128)S(1)} %lay.1.panel_ref.refs_4_.refs_2_.refs_6_.refs_8_.refs_10_.refs_12_.refs_14_, f32[2048,4096]{1,0:T(8,128)S(1)} %bitcast.3), custom_call_target="tpu_custom_call" | custom-call | flops 16777216 | tf_op jit(solution)/shard_map/first/pallas_call | solution.py:28
  15.0 0.2 collective-permute-start.4
  15.2 1.1 %collective-permute-done.4.b = f32[16,128]{1,0:T(8,128)S(1)} collective-permute-done((f32[16,128]{1,0:T(8,128)S(1)}, f32[16,128]{1,0:T(8,128)S(1)}, u32[]{:S(2)}, u32[]{:S(2)}) %collective-permute-start.4) | collective-permute-done | bytes 8224 | tf_op jit(solution)/shard_map/ppermute | solution.py:298
  16.2 2.7 %collective-permute-start.6 = (f32[16,128]{1,0:T(8,128)S(1)}, f32[16,128]{1,0:T(8,128)S(1)}, u32[]{:S(2)}, u32[]{:S(2)}) collective-permute-start(f32[16,128]{1,0:T(8,128)S(1)} %add.8.refs_0_), channel_id=1, source_target_pairs={{0,2},{1,3},{2,0},{3,1},{4,7},{5,6},{6,5},{7,4},{8,10},{9,11},{10,... | collective-permute-start | bytes 24584 | tf_op jit(solution)/shard_map/ppermute | solution.py:304
  19.0 1.6 %collective-permute-start.5 = (f32[16,128]{1,0:T(8,128)S(1)}, f32[16,128]{1,0:T(8,128)S(1)}, u32[]{:S(2)}, u32[]{:S(2)}) collective-permute-start(f32[16,128]{1,0:T(8,128)S(1)} %add.8.refs_0_), channel_id=1, source_target_pairs={{0,1},{1,0},{2,3},{3,2},{4,5},{5,4},{6,7},{7,6},{8,9},{9,8},{10,11... | collective-permute-start | bytes 24584 | tf_op jit(solution)/shard_map/ppermute | solution.py:301
  20.6 0.2 collective-permute-done.6.refs_2_
  20.9 1.7 %collective-permute-done.5.refs_1_ = f32[16,128]{1,0:T(8,128)S(1)} collective-permute-done((f32[16,128]{1,0:T(8,128)S(1)}, f32[16,128]{1,0:T(8,128)S(1)}, u32[]{:S(2)}, u32[]{:S(2)}) %collective-permute-start.5) | collective-permute-done | bytes 8224 | tf_op jit(solution)/shard_map/ppermute | solution.py:301
  22.7 3.1 %step1.1 = (f32[64,128]{1,0:T(8,128)S(1)}, f32[64,128]{1,0:T(8,128)S(1)}, f32[8,128]{1,0:T(8,128)S(1)}, f32[16,128]{1,0:T(8,128)S(1)}) custom-call(f32[16,128]{1,0:T(8,128)S(1)} %add.8.refs_0_, f32[16,128]{1,0:T(8,128)S(1)} %collective-permute-done.5.refs_1_, f32[16,128]{1,0:T(8,128)S(1)} %collective-permute-done.6.refs_2_, ...), custom_call_target="tpu_custom_call" | custom-call | flops 16777216 | tf_op jit(solution)/shard_map/step1/pallas_call | solution.py:28
  25.8 1.1 %collective-permute-done.8.b = f32[16,128]{1,0:T(8,128)S(1)} collective-permute-done((f32[16,128]{1,0:T(8,128)S(1)}, f32[16,128]{1,0:T(8,128)S(1)}, u32[]{:S(2)}, u32[]{:S(2)}) %collective-permute-start.8) | collective-permute-done | bytes 8224 | tf_op jit(solution)/shard_map/ppermute | solution.py:298
  27.0 2.1 %collective-permute-start.10 = (f32[16,128]{1,0:T(8,128)S(1)}, f32[16,128]{1,0:T(8,128)S(1)}, u32[]{:S(2)}, u32[]{:S(2)}) collective-permute-start(f32[16,128]{1,0:T(8,128)S(1)} %add.9.refs_0_), channel_id=1, source_target_pairs={{0,2},{1,3},{2,0},{3,1},{4,7},{5,6},{6,5},{7,4},{8,10},{9,11},{10,... | collective-permute-start | bytes 24584 | tf_op jit(solution)/shard_map/ppermute | solution.py:304
  29.0 1.6 %collective-permute-start.9 = (f32[16,128]{1,0:T(8,128)S(1)}, f32[16,128]{1,0:T(8,128)S(1)}, u32[]{:S(2)}, u32[]{:S(2)}) collective-permute-start(f32[16,128]{1,0:T(8,128)S(1)} %add.9.refs_0_), channel_id=1, source_target_pairs={{0,1},{1,0},{2,3},{3,2},{4,5},{5,4},{6,7},{7,6},{8,9},{9,8},{10,11... | collective-permute-start | bytes 24584 | tf_op jit(solution)/shard_map/ppermute | solution.py:301
  30.6 0.9 collective-permute-done.10.refs_2_
  31.6 1.0 collective-permute-done.9.refs_1_
  32.7 3.1 %step2.1 = (f32[64,128]{1,0:T(8,128)S(1)}, f32[64,128]{1,0:T(8,128)S(1)}, f32[8,128]{1,0:T(8,128)S(1)}, f32[16,128]{1,0:T(8,128)S(1)}) custom-call(f32[16,128]{1,0:T(8,128)S(1)} %add.9.refs_0_, f32[16,128]{1,0:T(8,128)S(1)} %collective-permute-done.9.refs_1_, f32[16,128]{1,0:T(8,128)S(1)} %collective-permute-done.10.refs_2_, ...), custom_call_target="tpu_custom_call" | custom-call | flops 16777216 | tf_op jit(solution)/shard_map/step2/pallas_call | solution.py:28
  35.8 0.2 collective-permute-start.12
  36.0 1.0 collective-permute-done.12.b
  37.0 2.0 %collective-permute-start.14 = (f32[16,128]{1,0:T(8,128)S(1)}, f32[16,128]{1,0:T(8,128)S(1)}, u32[]{:S(2)}, u32[]{:S(2)}) collective-permute-start(f32[16,128]{1,0:T(8,128)S(1)} %add.10.refs_0_), channel_id=1, source_target_pairs={{0,2},{1,3},{2,0},{3,1},{4,7},{5,6},{6,5},{7,4},{8,10},{9,11},{10,... | collective-permute-start | bytes 24584 | tf_op jit(solution)/shard_map/ppermute | solution.py:304
  39.1 1.6 %collective-permute-start.13 = (f32[16,128]{1,0:T(8,128)S(1)}, f32[16,128]{1,0:T(8,128)S(1)}, u32[]{:S(2)}, u32[]{:S(2)}) collective-permute-start(f32[16,128]{1,0:T(8,128)S(1)} %add.10.refs_0_), channel_id=1, source_target_pairs={{0,1},{1,0},{2,3},{3,2},{4,5},{5,4},{6,7},{7,6},{8,9},{9,8},{10,11... | collective-permute-start | bytes 24584 | tf_op jit(solution)/shard_map/ppermute | solution.py:301
  40.7 0.9 collective-permute-done.14.refs_2_
  41.7 1.1 %collective-permute-done.13.refs_1_ = f32[16,128]{1,0:T(8,128)S(1)} collective-permute-done((f32[16,128]{1,0:T(8,128)S(1)}, f32[16,128]{1,0:T(8,128)S(1)}, u32[]{:S(2)}, u32[]{:S(2)}) %collective-permute-start.13) | collective-permute-done | bytes 8224 | tf_op jit(solution)/shard_map/ppermute | solution.py:301
  42.8 3.1 %step3.1 = (f32[64,128]{1,0:T(8,128)S(1)}, f32[64,128]{1,0:T(8,128)S(1)}, f32[8,128]{1,0:T(8,128)S(1)}, f32[16,128]{1,0:T(8,128)S(1)}) custom-call(f32[16,128]{1,0:T(8,128)S(1)} %add.10.refs_0_, f32[16,128]{1,0:T(8,128)S(1)} %collective-permute-done.13.refs_1_, f32[16,128]{1,0:T(8,128)S(1)} %collective-permute-done.14.refs_2_, ...), custom_call_target="tpu_custom_call" | custom-call | flops 16777216 | tf_op jit(solution)/shard_map/step3/pallas_call | solution.py:28
  45.8 0.2 collective-permute-start.16
  46.0 1.1 %collective-permute-done.16.b = f32[16,128]{1,0:T(8,128)S(1)} collective-permute-done((f32[16,128]{1,0:T(8,128)S(1)}, f32[16,128]{1,0:T(8,128)S(1)}, u32[]{:S(2)}, u32[]{:S(2)}) %collective-permute-start.16) | collective-permute-done | bytes 8224 | tf_op jit(solution)/shard_map/ppermute | solution.py:298
  47.1 2.0 %collective-permute-start.18 = (f32[16,128]{1,0:T(8,128)S(1)}, f32[16,128]{1,0:T(8,128)S(1)}, u32[]{:S(2)}, u32[]{:S(2)}) collective-permute-start(f32[16,128]{1,0:T(8,128)S(1)} %add.11.refs_0_), channel_id=1, source_target_pairs={{0,2},{1,3},{2,0},{3,1},{4,7},{5,6},{6,5},{7,4},{8,10},{9,11},{10,... | collective-permute-start | bytes 24584 | tf_op jit(solution)/shard_map/ppermute | solution.py:304
  49.1 1.6 %collective-permute-start.17 = (f32[16,128]{1,0:T(8,128)S(1)}, f32[16,128]{1,0:T(8,128)S(1)}, u32[]{:S(2)}, u32[]{:S(2)}) collective-permute-start(f32[16,128]{1,0:T(8,128)S(1)} %add.11.refs_0_), channel_id=1, source_target_pairs={{0,1},{1,0},{2,3},{3,2},{4,5},{5,4},{6,7},{7,6},{8,9},{9,8},{10,11... | collective-permute-start | bytes 24584 | tf_op jit(solution)/shard_map/ppermute | solution.py:301
  50.7 0.9 collective-permute-done.18.refs_2_
  51.8 1.0 collective-permute-done.17.refs_1_
  52.8 3.1 %step4.1 = (f32[64,128]{1,0:T(8,128)S(1)}, f32[64,128]{1,0:T(8,128)S(1)}, f32[8,128]{1,0:T(8,128)S(1)}, f32[16,128]{1,0:T(8,128)S(1)}) custom-call(f32[16,128]{1,0:T(8,128)S(1)} %add.11.refs_0_, f32[16,128]{1,0:T(8,128)S(1)} %collective-permute-done.17.refs_1_, f32[16,128]{1,0:T(8,128)S(1)} %collective-permute-done.18.refs_2_, ...), custom_call_target="tpu_custom_call" | custom-call | flops 16777216 | tf_op jit(solution)/shard_map/step4/pallas_call | solution.py:28
  55.9 0.2 collective-permute-start.20
  56.1 1.0 collective-permute-done.20.b
  57.1 2.0 %collective-permute-start.22 = (f32[16,128]{1,0:T(8,128)S(1)}, f32[16,128]{1,0:T(8,128)S(1)}, u32[]{:S(2)}, u32[]{:S(2)}) collective-permute-start(f32[16,128]{1,0:T(8,128)S(1)} %add.12.refs_0_), channel_id=1, source_target_pairs={{0,2},{1,3},{2,0},{3,1},{4,7},{5,6},{6,5},{7,4},{8,10},{9,11},{10,... | collective-permute-start | bytes 24584 | tf_op jit(solution)/shard_map/ppermute | solution.py:304
  59.1 1.7 %collective-permute-start.21 = (f32[16,128]{1,0:T(8,128)S(1)}, f32[16,128]{1,0:T(8,128)S(1)}, u32[]{:S(2)}, u32[]{:S(2)}) collective-permute-start(f32[16,128]{1,0:T(8,128)S(1)} %add.12.refs_0_), channel_id=1, source_target_pairs={{0,1},{1,0},{2,3},{3,2},{4,5},{5,4},{6,7},{7,6},{8,9},{9,8},{10,11... | collective-permute-start | bytes 24584 | tf_op jit(solution)/shard_map/ppermute | solution.py:301
  60.8 0.9 collective-permute-done.22.refs_2_
  61.8 1.0 collective-permute-done.21.refs_1_
  62.8 3.1 %step5.1 = (f32[64,128]{1,0:T(8,128)S(1)}, f32[64,128]{1,0:T(8,128)S(1)}, f32[8,128]{1,0:T(8,128)S(1)}, f32[16,128]{1,0:T(8,128)S(1)}) custom-call(f32[16,128]{1,0:T(8,128)S(1)} %add.12.refs_0_, f32[16,128]{1,0:T(8,128)S(1)} %collective-permute-done.21.refs_1_, f32[16,128]{1,0:T(8,128)S(1)} %collective-permute-done.22.refs_2_, ...), custom_call_target="tpu_custom_call" | custom-call | flops 16777216 | tf_op jit(solution)/shard_map/step5/pallas_call | solution.py:28
  65.9 0.2 collective-permute-start.24
  66.1 1.0 collective-permute-done.24.b
  67.2 2.0 %collective-permute-start.26 = (f32[16,128]{1,0:T(8,128)S(1)}, f32[16,128]{1,0:T(8,128)S(1)}, u32[]{:S(2)}, u32[]{:S(2)}) collective-permute-start(f32[16,128]{1,0:T(8,128)S(1)} %add.13.refs_0_), channel_id=1, source_target_pairs={{0,2},{1,3},{2,0},{3,1},{4,7},{5,6},{6,5},{7,4},{8,10},{9,11},{10,... | collective-permute-start | bytes 24584 | tf_op jit(solution)/shard_map/ppermute | solution.py:304
  69.2 1.7 %collective-permute-start.25 = (f32[16,128]{1,0:T(8,128)S(1)}, f32[16,128]{1,0:T(8,128)S(1)}, u32[]{:S(2)}, u32[]{:S(2)}) collective-permute-start(f32[16,128]{1,0:T(8,128)S(1)} %add.13.refs_0_), channel_id=1, source_target_pairs={{0,1},{1,0},{2,3},{3,2},{4,5},{5,4},{6,7},{7,6},{8,9},{9,8},{10,11... | collective-permute-start | bytes 24584 | tf_op jit(solution)/shard_map/ppermute | solution.py:301
  70.8 0.9 collective-permute-done.26.refs_2_
  71.9 1.0 collective-permute-done.25.refs_1_
  72.9 3.1 %step6.1 = (f32[64,128]{1,0:T(8,128)S(1)}, f32[64,128]{1,0:T(8,128)S(1)}, f32[8,128]{1,0:T(8,128)S(1)}, f32[16,128]{1,0:T(8,128)S(1)}) custom-call(f32[16,128]{1,0:T(8,128)S(1)} %add.13.refs_0_, f32[16,128]{1,0:T(8,128)S(1)} %collective-permute-done.25.refs_1_, f32[16,128]{1,0:T(8,128)S(1)} %collective-permute-done.26.refs_2_, ...), custom_call_target="tpu_custom_call" | custom-call | flops 16777216 | tf_op jit(solution)/shard_map/step6/pallas_call | solution.py:28
  75.9 0.2 collective-permute-start.28
  76.2 1.0 collective-permute-done.28.b
  77.2 2.0 %collective-permute-start.30 = (f32[16,128]{1,0:T(8,128)S(1)}, f32[16,128]{1,0:T(8,128)S(1)}, u32[]{:S(2)}, u32[]{:S(2)}) collective-permute-start(f32[16,128]{1,0:T(8,128)S(1)} %add.14.refs_0_), channel_id=1, source_target_pairs={{0,2},{1,3},{2,0},{3,1},{4,7},{5,6},{6,5},{7,4},{8,10},{9,11},{10,... | collective-permute-start | bytes 24584 | tf_op jit(solution)/shard_map/ppermute | solution.py:304
  79.2 1.7 %collective-permute-start.29 = (f32[16,128]{1,0:T(8,128)S(1)}, f32[16,128]{1,0:T(8,128)S(1)}, u32[]{:S(2)}, u32[]{:S(2)}) collective-permute-start(f32[16,128]{1,0:T(8,128)S(1)} %add.14.refs_0_), channel_id=1, source_target_pairs={{0,1},{1,0},{2,3},{3,2},{4,5},{5,4},{6,7},{7,6},{8,9},{9,8},{10,11... | collective-permute-start | bytes 24584 | tf_op jit(solution)/shard_map/ppermute | solution.py:301
  80.9 0.8 collective-permute-done.30.refs_2_
  81.7 0.2 between6.1
  81.9 1.0 collective-permute-done.29.refs_1_
  82.9 3.1 %step7.1 = (f32[64,128]{1,0:T(8,128)S(1)}, f32[64,128]{1,0:T(8,128)S(1)}, f32[8,128]{1,0:T(8,128)S(1)}, f32[16,128]{1,0:T(8,128)S(1)}) custom-call(f32[16,128]{1,0:T(8,128)S(1)} %add.14.refs_0_, f32[16,128]{1,0:T(8,128)S(1)} %collective-permute-done.29.refs_1_, f32[16,128]{1,0:T(8,128)S(1)} %collective-permute-done.30.refs_2_, ...), custom_call_target="tpu_custom_call" | custom-call | flops 16777216 | tf_op jit(solution)/shard_map/step7/pallas_call | solution.py:28
  86.0 0.2 collective-permute-start.32
  86.2 1.0 collective-permute-done.32.b
  87.2 2.0 %collective-permute-start.34 = (f32[16,128]{1,0:T(8,128)S(1)}, f32[16,128]{1,0:T(8,128)S(1)}, u32[]{:S(2)}, u32[]{:S(2)}) collective-permute-start(f32[16,128]{1,0:T(8,128)S(1)} %add.15.refs_0_), channel_id=1, source_target_pairs={{0,2},{1,3},{2,0},{3,1},{4,7},{5,6},{6,5},{7,4},{8,10},{9,11},{10,... | collective-permute-start | bytes 24584 | tf_op jit(solution)/shard_map/ppermute | solution.py:304
  89.2 1.7 %collective-permute-start.33 = (f32[16,128]{1,0:T(8,128)S(1)}, f32[16,128]{1,0:T(8,128)S(1)}, u32[]{:S(2)}, u32[]{:S(2)}) collective-permute-start(f32[16,128]{1,0:T(8,128)S(1)} %add.15.refs_0_), channel_id=1, source_target_pairs={{0,1},{1,0},{2,3},{3,2},{4,5},{5,4},{6,7},{7,6},{8,9},{9,8},{10,11... | collective-permute-start | bytes 24584 | tf_op jit(solution)/shard_map/ppermute | solution.py:301
  90.9 0.8 collective-permute-done.34.refs_2_
  91.9 1.0 collective-permute-done.33.refs_1_
  92.9 12.2 %last.1 = f32[2048,4096]{1,0:T(8,128)} custom-call(f32[16,128]{1,0:T(8,128)S(1)} %add.15.refs_0_, f32[16,128]{1,0:T(8,128)S(1)} %collective-permute-done.33.refs_1_, f32[16,128]{1,0:T(8,128)S(1)} %collective-permute-done.34.refs_2_, f32[16,128]{1,0:T(8,128)S(1)} %collective-permute-done.35.refs_3_, f32[64,128]{1,0:T(8,128)S(1)} %get-tuple-element.49.refs_5_.refs_0_.refs_4_, ...), custom_call_target="tpu_custom_call" | custom-call | flops 268435456 | bytes 67108864 | tf_op jit(solution)/shard_map/last/pallas_call | solution.py:378
  (37 shorter events, 1.3 us)
Async XLA Ops:
  0.0 12.2 %copy-start = (f32[1,2048,4096]{2,1,0:T(8,128)S(1)}, f32[1,2048,4096]{2,1,0:T(8,128)}, u32[]{:S(2)}) copy-start(f32[1,2048,4096]{2,1,0:T(8,128)} %param.1) | copy-start | bytes 100663296
  1.7 1.5 %collective-permute-start = (f32[128,128]{1,0:T(8,128)S(1)}, f32[128,128]{1,0:T(8,128)S(1)}, u32[]{:S(2)}, u32[]{:S(2)}) collective-permute-start(f32[128,128]{1,0:T(8,128)S(1)} %panel.1.own), channel_id=1, source_target_pairs={{0,4},{4,0},{1,5},{5,1},{2,6},{6,2},{3,7},{7,3},{8,12},{12,8},{9,1... | collective-permute-start | bytes 196616 | tf_op jit(solution)/shard_map/ppermute | solution.py:298
  3.2 7.7 %collective-permute-start.2 = (f32[128,128]{1,0:T(8,128)S(1)}, f32[128,128]{1,0:T(8,128)S(1)}, u32[]{:S(2)}, u32[]{:S(2)}) collective-permute-start(f32[128,128]{1,0:T(8,128)S(1)} %pick.1.refs_0_), channel_id=1, source_target_pairs={{0,2},{1,3},{2,0},{3,1},{4,7},{5,6},{6,5},{7,4},{8,10},{9,11},{10,... | collective-permute-start | bytes 196616 | tf_op jit(solution)/shard_map/ppermute | solution.py:304
  7.2 5.0 %collective-permute-start.1 = (f32[128,128]{1,0:T(8,128)S(1)}, f32[128,128]{1,0:T(8,128)S(1)}, u32[]{:S(2)}, u32[]{:S(2)}) collective-permute-start(f32[128,128]{1,0:T(8,128)S(1)} %pick.1.refs_0_), channel_id=1, source_target_pairs={{0,1},{1,0},{2,3},{3,2},{4,5},{5,4},{6,7},{7,6},{8,9},{9,8},{10,11... | collective-permute-start | bytes 196616 | tf_op jit(solution)/shard_map/ppermute | solution.py:301
  10.8 1.3 %collective-permute-start.3 = (f32[128,128]{1,0:T(8,128)S(1)}, f32[128,128]{1,0:T(8,128)S(1)}, u32[]{:S(2)}, u32[]{:S(2)}) collective-permute-start(f32[128,128]{1,0:T(8,128)S(1)} %collective-permute-done.2.refs_2_), channel_id=1, source_target_pairs={{0,4},{4,0},{1,5},{5,1},{2,6},{6,2},{3,7},{7,3},{8,12},{12,8},{9,1... | collective-permute-start | bytes 196616 | tf_op jit(solution)/shard_map/ppermute | solution.py:298
  15.0 1.2 %collective-permute-start.4 = (f32[16,128]{1,0:T(8,128)S(1)}, f32[16,128]{1,0:T(8,128)S(1)}, u32[]{:S(2)}, u32[]{:S(2)}) collective-permute-start(f32[16,128]{1,0:T(8,128)S(1)} %get-tuple-element.48.a), channel_id=1, source_target_pairs={{0,4},{4,0},{1,5},{5,1},{2,6},{6,2},{3,7},{7,3},{8,12},{12,8},{9,1... | collective-permute-start | bytes 24584 | tf_op jit(solution)/shard_map/ppermute | solution.py:298
  16.2 4.5 %collective-permute-start.6 = (f32[16,128]{1,0:T(8,128)S(1)}, f32[16,128]{1,0:T(8,128)S(1)}, u32[]{:S(2)}, u32[]{:S(2)}) collective-permute-start(f32[16,128]{1,0:T(8,128)S(1)} %add.8.refs_0_), channel_id=1, source_target_pairs={{0,2},{1,3},{2,0},{3,1},{4,7},{5,6},{6,5},{7,4},{8,10},{9,11},{10,... | collective-permute-start | bytes 24584 | tf_op jit(solution)/shard_map/ppermute | solution.py:304
  19.0 3.7 %collective-permute-start.5 = (f32[16,128]{1,0:T(8,128)S(1)}, f32[16,128]{1,0:T(8,128)S(1)}, u32[]{:S(2)}, u32[]{:S(2)}) collective-permute-start(f32[16,128]{1,0:T(8,128)S(1)} %add.8.refs_0_), channel_id=1, source_target_pairs={{0,1},{1,0},{2,3},{3,2},{4,5},{5,4},{6,7},{7,6},{8,9},{9,8},{10,11... | collective-permute-start | bytes 24584 | tf_op jit(solution)/shard_map/ppermute | solution.py:301
  20.8 1.9 %collective-permute-start.7 = (f32[16,128]{1,0:T(8,128)S(1)}, f32[16,128]{1,0:T(8,128)S(1)}, u32[]{:S(2)}, u32[]{:S(2)}) collective-permute-start(f32[16,128]{1,0:T(8,128)S(1)} %collective-permute-done.6.refs_2_), channel_id=1, source_target_pairs={{0,4},{4,0},{1,5},{5,1},{2,6},{6,2},{3,7},{7,3},{8,12},{12,8},{9,1... | collective-permute-start | bytes 24584 | tf_op jit(solution)/shard_map/ppermute | solution.py:298
  25.7 1.2 %collective-permute-start.8 = (f32[16,128]{1,0:T(8,128)S(1)}, f32[16,128]{1,0:T(8,128)S(1)}, u32[]{:S(2)}, u32[]{:S(2)}) collective-permute-start(f32[16,128]{1,0:T(8,128)S(1)} %get-tuple-element.51.a), channel_id=1, source_target_pairs={{0,4},{4,0},{1,5},{5,1},{2,6},{6,2},{3,7},{7,3},{8,12},{12,8},{9,1... | collective-permute-start | bytes 24584 | tf_op jit(solution)/shard_map/ppermute | solution.py:298
  27.0 4.5 %collective-permute-start.10 = (f32[16,128]{1,0:T(8,128)S(1)}, f32[16,128]{1,0:T(8,128)S(1)}, u32[]{:S(2)}, u32[]{:S(2)}) collective-permute-start(f32[16,128]{1,0:T(8,128)S(1)} %add.9.refs_0_), channel_id=1, source_target_pairs={{0,2},{1,3},{2,0},{3,1},{4,7},{5,6},{6,5},{7,4},{8,10},{9,11},{10,... | collective-permute-start | bytes 24584 | tf_op jit(solution)/shard_map/ppermute | solution.py:304
  29.0 3.7 %collective-permute-start.9 = (f32[16,128]{1,0:T(8,128)S(1)}, f32[16,128]{1,0:T(8,128)S(1)}, u32[]{:S(2)}, u32[]{:S(2)}) collective-permute-start(f32[16,128]{1,0:T(8,128)S(1)} %add.9.refs_0_), channel_id=1, source_target_pairs={{0,1},{1,0},{2,3},{3,2},{4,5},{5,4},{6,7},{7,6},{8,9},{9,8},{10,11... | collective-permute-start | bytes 24584 | tf_op jit(solution)/shard_map/ppermute | solution.py:301
  31.5 1.2 %collective-permute-start.11 = (f32[16,128]{1,0:T(8,128)S(1)}, f32[16,128]{1,0:T(8,128)S(1)}, u32[]{:S(2)}, u32[]{:S(2)}) collective-permute-start(f32[16,128]{1,0:T(8,128)S(1)} %collective-permute-done.10.refs_2_), channel_id=1, source_target_pairs={{0,4},{4,0},{1,5},{5,1},{2,6},{6,2},{3,7},{7,3},{8,12},{12,8},{9,1... | collective-permute-start | bytes 24584 | tf_op jit(solution)/shard_map/ppermute | solution.py:298
  35.8 1.2 %collective-permute-start.12 = (f32[16,128]{1,0:T(8,128)S(1)}, f32[16,128]{1,0:T(8,128)S(1)}, u32[]{:S(2)}, u32[]{:S(2)}) collective-permute-start(f32[16,128]{1,0:T(8,128)S(1)} %get-tuple-element.57.a), channel_id=1, source_target_pairs={{0,4},{4,0},{1,5},{5,1},{2,6},{6,2},{3,7},{7,3},{8,12},{12,8},{9,1... | collective-permute-start | bytes 24584 | tf_op jit(solution)/shard_map/ppermute | solution.py:298
  37.0 4.5 %collective-permute-start.14 = (f32[16,128]{1,0:T(8,128)S(1)}, f32[16,128]{1,0:T(8,128)S(1)}, u32[]{:S(2)}, u32[]{:S(2)}) collective-permute-start(f32[16,128]{1,0:T(8,128)S(1)} %add.10.refs_0_), channel_id=1, source_target_pairs={{0,2},{1,3},{2,0},{3,1},{4,7},{5,6},{6,5},{7,4},{8,10},{9,11},{10,... | collective-permute-start | bytes 24584 | tf_op jit(solution)/shard_map/ppermute | solution.py:304
  39.1 3.7 %collective-permute-start.13 = (f32[16,128]{1,0:T(8,128)S(1)}, f32[16,128]{1,0:T(8,128)S(1)}, u32[]{:S(2)}, u32[]{:S(2)}) collective-permute-start(f32[16,128]{1,0:T(8,128)S(1)} %add.10.refs_0_), channel_id=1, source_target_pairs={{0,1},{1,0},{2,3},{3,2},{4,5},{5,4},{6,7},{7,6},{8,9},{9,8},{10,11... | collective-permute-start | bytes 24584 | tf_op jit(solution)/shard_map/ppermute | solution.py:301
  41.6 1.2 %collective-permute-start.15 = (f32[16,128]{1,0:T(8,128)S(1)}, f32[16,128]{1,0:T(8,128)S(1)}, u32[]{:S(2)}, u32[]{:S(2)}) collective-permute-start(f32[16,128]{1,0:T(8,128)S(1)} %collective-permute-done.14.refs_2_), channel_id=1, source_target_pairs={{0,4},{4,0},{1,5},{5,1},{2,6},{6,2},{3,7},{7,3},{8,12},{12,8},{9,1... | collective-permute-start | bytes 24584 | tf_op jit(solution)/shard_map/ppermute | solution.py:298
  45.8 1.2 %collective-permute-start.16 = (f32[16,128]{1,0:T(8,128)S(1)}, f32[16,128]{1,0:T(8,128)S(1)}, u32[]{:S(2)}, u32[]{:S(2)}) collective-permute-start(f32[16,128]{1,0:T(8,128)S(1)} %get-tuple-element.63.a), channel_id=1, source_target_pairs={{0,4},{4,0},{1,5},{5,1},{2,6},{6,2},{3,7},{7,3},{8,12},{12,8},{9,1... | collective-permute-start | bytes 24584 | tf_op jit(solution)/shard_map/ppermute | solution.py:298
  47.1 4.5 %collective-permute-start.18 = (f32[16,128]{1,0:T(8,128)S(1)}, f32[16,128]{1,0:T(8,128)S(1)}, u32[]{:S(2)}, u32[]{:S(2)}) collective-permute-start(f32[16,128]{1,0:T(8,128)S(1)} %add.11.refs_0_), channel_id=1, source_target_pairs={{0,2},{1,3},{2,0},{3,1},{4,7},{5,6},{6,5},{7,4},{8,10},{9,11},{10,... | collective-permute-start | bytes 24584 | tf_op jit(solution)/shard_map/ppermute | solution.py:304
  49.1 3.7 %collective-permute-start.17 = (f32[16,128]{1,0:T(8,128)S(1)}, f32[16,128]{1,0:T(8,128)S(1)}, u32[]{:S(2)}, u32[]{:S(2)}) collective-permute-start(f32[16,128]{1,0:T(8,128)S(1)} %add.11.refs_0_), channel_id=1, source_target_pairs={{0,1},{1,0},{2,3},{3,2},{4,5},{5,4},{6,7},{7,6},{8,9},{9,8},{10,11... | collective-permute-start | bytes 24584 | tf_op jit(solution)/shard_map/ppermute | solution.py:301
  51.6 1.2 %collective-permute-start.19 = (f32[16,128]{1,0:T(8,128)S(1)}, f32[16,128]{1,0:T(8,128)S(1)}, u32[]{:S(2)}, u32[]{:S(2)}) collective-permute-start(f32[16,128]{1,0:T(8,128)S(1)} %collective-permute-done.18.refs_2_), channel_id=1, source_target_pairs={{0,4},{4,0},{1,5},{5,1},{2,6},{6,2},{3,7},{7,3},{8,12},{12,8},{9,1... | collective-permute-start | bytes 24584 | tf_op jit(solution)/shard_map/ppermute | solution.py:298
  55.9 1.2 %collective-permute-start.20 = (f32[16,128]{1,0:T(8,128)S(1)}, f32[16,128]{1,0:T(8,128)S(1)}, u32[]{:S(2)}, u32[]{:S(2)}) collective-permute-start(f32[16,128]{1,0:T(8,128)S(1)} %get-tuple-element.69.a), channel_id=1, source_target_pairs={{0,4},{4,0},{1,5},{5,1},{2,6},{6,2},{3,7},{7,3},{8,12},{12,8},{9,1... | collective-permute-start | bytes 24584 | tf_op jit(solution)/shard_map/ppermute | solution.py:298
  57.1 4.5 %collective-permute-start.22 = (f32[16,128]{1,0:T(8,128)S(1)}, f32[16,128]{1,0:T(8,128)S(1)}, u32[]{:S(2)}, u32[]{:S(2)}) collective-permute-start(f32[16,128]{1,0:T(8,128)S(1)} %add.12.refs_0_), channel_id=1, source_target_pairs={{0,2},{1,3},{2,0},{3,1},{4,7},{5,6},{6,5},{7,4},{8,10},{9,11},{10,... | collective-permute-start | bytes 24584 | tf_op jit(solution)/shard_map/ppermute | solution.py:304
  59.1 3.7 %collective-permute-start.21 = (f32[16,128]{1,0:T(8,128)S(1)}, f32[16,128]{1,0:T(8,128)S(1)}, u32[]{:S(2)}, u32[]{:S(2)}) collective-permute-start(f32[16,128]{1,0:T(8,128)S(1)} %add.12.refs_0_), channel_id=1, source_target_pairs={{0,1},{1,0},{2,3},{3,2},{4,5},{5,4},{6,7},{7,6},{8,9},{9,8},{10,11... | collective-permute-start | bytes 24584 | tf_op jit(solution)/shard_map/ppermute | solution.py:301
  61.7 1.2 %collective-permute-start.23 = (f32[16,128]{1,0:T(8,128)S(1)}, f32[16,128]{1,0:T(8,128)S(1)}, u32[]{:S(2)}, u32[]{:S(2)}) collective-permute-start(f32[16,128]{1,0:T(8,128)S(1)} %collective-permute-done.22.refs_2_), channel_id=1, source_target_pairs={{0,4},{4,0},{1,5},{5,1},{2,6},{6,2},{3,7},{7,3},{8,12},{12,8},{9,1... | collective-permute-start | bytes 24584 | tf_op jit(solution)/shard_map/ppermute | solution.py:298
  65.9 1.2 %collective-permute-start.24 = (f32[16,128]{1,0:T(8,128)S(1)}, f32[16,128]{1,0:T(8,128)S(1)}, u32[]{:S(2)}, u32[]{:S(2)}) collective-permute-start(f32[16,128]{1,0:T(8,128)S(1)} %get-tuple-element.75.a), channel_id=1, source_target_pairs={{0,4},{4,0},{1,5},{5,1},{2,6},{6,2},{3,7},{7,3},{8,12},{12,8},{9,1... | collective-permute-start | bytes 24584 | tf_op jit(solution)/shard_map/ppermute | solution.py:298
  67.2 4.5 %collective-permute-start.26 = (f32[16,128]{1,0:T(8,128)S(1)}, f32[16,128]{1,0:T(8,128)S(1)}, u32[]{:S(2)}, u32[]{:S(2)}) collective-permute-start(f32[16,128]{1,0:T(8,128)S(1)} %add.13.refs_0_), channel_id=1, source_target_pairs={{0,2},{1,3},{2,0},{3,1},{4,7},{5,6},{6,5},{7,4},{8,10},{9,11},{10,... | collective-permute-start | bytes 24584 | tf_op jit(solution)/shard_map/ppermute | solution.py:304
  69.2 3.7 %collective-permute-start.25 = (f32[16,128]{1,0:T(8,128)S(1)}, f32[16,128]{1,0:T(8,128)S(1)}, u32[]{:S(2)}, u32[]{:S(2)}) collective-permute-start(f32[16,128]{1,0:T(8,128)S(1)} %add.13.refs_0_), channel_id=1, source_target_pairs={{0,1},{1,0},{2,3},{3,2},{4,5},{5,4},{6,7},{7,6},{8,9},{9,8},{10,11... | collective-permute-start | bytes 24584 | tf_op jit(solution)/shard_map/ppermute | solution.py:301
  71.7 1.2 %collective-permute-start.27 = (f32[16,128]{1,0:T(8,128)S(1)}, f32[16,128]{1,0:T(8,128)S(1)}, u32[]{:S(2)}, u32[]{:S(2)}) collective-permute-start(f32[16,128]{1,0:T(8,128)S(1)} %collective-permute-done.26.refs_2_), channel_id=1, source_target_pairs={{0,4},{4,0},{1,5},{5,1},{2,6},{6,2},{3,7},{7,3},{8,12},{12,8},{9,1... | collective-permute-start | bytes 24584 | tf_op jit(solution)/shard_map/ppermute | solution.py:298
  75.9 1.2 %collective-permute-start.28 = (f32[16,128]{1,0:T(8,128)S(1)}, f32[16,128]{1,0:T(8,128)S(1)}, u32[]{:S(2)}, u32[]{:S(2)}) collective-permute-start(f32[16,128]{1,0:T(8,128)S(1)} %get-tuple-element.81.a), channel_id=1, source_target_pairs={{0,4},{4,0},{1,5},{5,1},{2,6},{6,2},{3,7},{7,3},{8,12},{12,8},{9,1... | collective-permute-start | bytes 24584 | tf_op jit(solution)/shard_map/ppermute | solution.py:298
  77.2 4.5 %collective-permute-start.30 = (f32[16,128]{1,0:T(8,128)S(1)}, f32[16,128]{1,0:T(8,128)S(1)}, u32[]{:S(2)}, u32[]{:S(2)}) collective-permute-start(f32[16,128]{1,0:T(8,128)S(1)} %add.14.refs_0_), channel_id=1, source_target_pairs={{0,2},{1,3},{2,0},{3,1},{4,7},{5,6},{6,5},{7,4},{8,10},{9,11},{10,... | collective-permute-start | bytes 24584 | tf_op jit(solution)/shard_map/ppermute | solution.py:304
  79.2 3.7 %collective-permute-start.29 = (f32[16,128]{1,0:T(8,128)S(1)}, f32[16,128]{1,0:T(8,128)S(1)}, u32[]{:S(2)}, u32[]{:S(2)}) collective-permute-start(f32[16,128]{1,0:T(8,128)S(1)} %add.14.refs_0_), channel_id=1, source_target_pairs={{0,1},{1,0},{2,3},{3,2},{4,5},{5,4},{6,7},{7,6},{8,9},{9,8},{10,11... | collective-permute-start | bytes 24584 | tf_op jit(solution)/shard_map/ppermute | solution.py:301
  81.7 1.2 %collective-permute-start.31 = (f32[16,128]{1,0:T(8,128)S(1)}, f32[16,128]{1,0:T(8,128)S(1)}, u32[]{:S(2)}, u32[]{:S(2)}) collective-permute-start(f32[16,128]{1,0:T(8,128)S(1)} %collective-permute-done.30.refs_2_), channel_id=1, source_target_pairs={{0,4},{4,0},{1,5},{5,1},{2,6},{6,2},{3,7},{7,3},{8,12},{12,8},{9,1... | collective-permute-start | bytes 24584 | tf_op jit(solution)/shard_map/ppermute | solution.py:298
  86.0 1.2 %collective-permute-start.32 = (f32[16,128]{1,0:T(8,128)S(1)}, f32[16,128]{1,0:T(8,128)S(1)}, u32[]{:S(2)}, u32[]{:S(2)}) collective-permute-start(f32[16,128]{1,0:T(8,128)S(1)} %get-tuple-element.87.a), channel_id=1, source_target_pairs={{0,4},{4,0},{1,5},{5,1},{2,6},{6,2},{3,7},{7,3},{8,12},{12,8},{9,1... | collective-permute-start | bytes 24584 | tf_op jit(solution)/shard_map/ppermute | solution.py:298
  87.2 4.5 %collective-permute-start.34 = (f32[16,128]{1,0:T(8,128)S(1)}, f32[16,128]{1,0:T(8,128)S(1)}, u32[]{:S(2)}, u32[]{:S(2)}) collective-permute-start(f32[16,128]{1,0:T(8,128)S(1)} %add.15.refs_0_), channel_id=1, source_target_pairs={{0,2},{1,3},{2,0},{3,1},{4,7},{5,6},{6,5},{7,4},{8,10},{9,11},{10,... | collective-permute-start | bytes 24584 | tf_op jit(solution)/shard_map/ppermute | solution.py:304
  89.2 3.7 %collective-permute-start.33 = (f32[16,128]{1,0:T(8,128)S(1)}, f32[16,128]{1,0:T(8,128)S(1)}, u32[]{:S(2)}, u32[]{:S(2)}) collective-permute-start(f32[16,128]{1,0:T(8,128)S(1)} %add.15.refs_0_), channel_id=1, source_target_pairs={{0,1},{1,0},{2,3},{3,2},{4,5},{5,4},{6,7},{7,6},{8,9},{9,8},{10,11... | collective-permute-start | bytes 24584 | tf_op jit(solution)/shard_map/ppermute | solution.py:301
  91.8 1.2 %collective-permute-start.35 = (f32[16,128]{1,0:T(8,128)S(1)}, f32[16,128]{1,0:T(8,128)S(1)}, u32[]{:S(2)}, u32[]{:S(2)}) collective-permute-start(f32[16,128]{1,0:T(8,128)S(1)} %collective-permute-done.34.refs_2_), channel_id=1, source_target_pairs={{0,4},{4,0},{1,5},{5,1},{2,6},{6,2},{3,7},{7,3},{8,12},{12,8},{9,1... | collective-permute-start | bytes 24584 | tf_op jit(solution)/shard_map/ppermute | solution.py:298
